TPU v7x, 8 devices: a whole 2x2x1 slice. The times are simulated.
8 devices in a mesh: data: 1 (over z), col: 2 (over y), row: 4 (over x, core).
Axes of the slice: x: 2, y: 2, z: 1, core: 2. Of those that a mesh axis runs over, the one named last changes fastest.
Arguments:
- x_seq: bfloat16 [64, 8, 2560], P(None, 'data', 'row')
- h_init: float32 [2, 8, 2560], P(None, 'data', 'row')
- wx_l1: bfloat16 [2560, 3, 2560], P('row', None, 'col')
- whru_l1: bfloat16 [2560, 2, 2560], P('row', None, 'col')
- whn_l1: bfloat16 [2560, 2560], P('row', 'col')
- bias_l1: float32 [3, 2560], P(None, 'col')
- wx_l2: bfloat16 [2560, 3, 2560], P('row', None, 'col')
- whru_l2: bfloat16 [2560, 2, 2560], P('row', None, 'col')
- whn_l2: bfloat16 [2560, 2560], P('row', 'col')
- bias_l2: float32 [3, 2560], P(None, 'col')
Outputs:
- output 1: bfloat16 [64, 8, 2560], P(None, 'data', ('col', 'row'))
- output 2: float32 [2, 8, 2560], P(None, 'data', ('col', 'row'))
All inputs are finite; a program needn't handle non-finite values.
Results may differ from a plain program's by a relative error of at most 0.00269291.
Values are sent between devices in bfloat16 or wider.
A program may use at most 1 GiB of HBM per device.

v0:
```python
import jax
import jax.numpy as jnp
from jax import lax
from jax.sharding import PartitionSpec as P


def solution(mesh):
    row_count = mesh.shape["row"]
    seq_spec = P(None, "data", "row")
    out_spec = P(None, "data", ("col", "row"))
    wide_spec = P("row", None, "col")
    square_spec = P("row", "col")
    bias_spec = P(None, "col")

    def gather_rows(col_part, row_idx, row_block):
        gathered = lax.all_gather(col_part, "col", axis=1, tiled=True)
        return lax.dynamic_slice_in_dim(gathered, row_idx * row_block, row_block, axis=1)

    def own_part(col_part, row_idx):
        unit_block = col_part.shape[-1] // row_count
        return lax.dynamic_slice_in_dim(col_part, row_idx * unit_block, unit_block, axis=col_part.ndim - 1)

    def gru_layer(in_rows, h_col, h_row, w_x, w_hru, w_hn, gate_bias, keep_rows):
        row_idx = lax.axis_index("row")
        row_block = in_rows.shape[2]

        def gru_step(state_pair, step_in):
            h_prev, prev_row = state_pair
            in_part = jnp.einsum("bk,kgn->bgn", step_in, w_x, preferred_element_type=jnp.float32)
            rec_part = jnp.einsum("bk,kgn->bgn", prev_row, w_hru, preferred_element_type=jnp.float32)
            part_sum = jnp.concatenate([in_part[:, :2] + rec_part, in_part[:, 2:]], axis=1)
            gate_pre = lax.psum(part_sum, "row") + gate_bias
            reset_gate = jax.nn.sigmoid(gate_pre[:, 0])
            update_gate = jax.nn.sigmoid(gate_pre[:, 1])
            gated_row = gather_rows((reset_gate * h_prev).astype(jnp.bfloat16), row_idx, row_block)
            cand_pre = lax.psum(jnp.dot(gated_row, w_hn, preferred_element_type=jnp.float32), "row")
            candidate = jnp.tanh(gate_pre[:, 2] + cand_pre)
            h_next = (1.0 - update_gate) * candidate + update_gate * h_prev
            next_row = gather_rows(h_next.astype(jnp.bfloat16), row_idx, row_block)
            if keep_rows:
                step_out = next_row
            else:
                step_out = own_part(h_next, row_idx).astype(jnp.bfloat16)
            return (h_next, next_row), step_out

        final_pair, seq_out = lax.scan(gru_step, (h_col, h_row), in_rows)
        return final_pair[0], seq_out

    def device_body(x_rows, h_rows, wx_l1, whru_l1, whn_l1, bias_l1, wx_l2, whru_l2, whn_l2, bias_l2):
        row_idx = lax.axis_index("row")
        col_idx = lax.axis_index("col")
        col_block = wx_l1.shape[2]
        h_gathered = lax.all_gather(h_rows, "row", axis=2, tiled=True)
        h_cols = lax.dynamic_slice_in_dim(h_gathered, col_idx * col_block, col_block, axis=2)
        h_starts = h_rows.astype(jnp.bfloat16)
        h1_last, h1_rows = gru_layer(x_rows, h_cols[0], h_starts[0], wx_l1, whru_l1, whn_l1, bias_l1, True)
        h2_last, h2_own = gru_layer(h1_rows, h_cols[1], h_starts[1], wx_l2, whru_l2, whn_l2, bias_l2, False)
        h_final = jnp.stack([own_part(h1_last, row_idx), own_part(h2_last, row_idx)])
        return h2_own, h_final

    return jax.shard_map(
        device_body,
        mesh=mesh,
        in_specs=(seq_spec, seq_spec, wide_spec, wide_spec, square_spec, bias_spec, wide_spec, wide_spec, square_spec, bias_spec),
        out_specs=(out_spec, out_spec),
        check_vma=False,
    )
```

profile of v0, /device:TPU:0, one launch (start us, length us, event | category | flops | bytes accessed | tf_op | source)
XLA Modules:
  0.0 7080.3 jit_solution(6268825159482029797)
XLA Ops:
  20.7 3522.3 %while.32 = (s32[]{:T(128)}, f32[8,1280]{1,0:T(8,128)S(1)}, bf16[8,640]{1,0:T(8,128)(2,1)S(1)}, bf16[64,8,640]{2,1,0:T(8,128)(2,1)}, bf16[64,8,640]{2,1,0:T(8,12...) while((s32[]{:T(128)}, f32[8,1280]{1,0:T(8,128)S(1)}, ...), condition=%wide.region_3.4_spmd, body=%wide.region_0.3_spmd.sunk | while | flops 78909440 | bytes 12078761 | solution.py:46
  3545.4 3527.4 %while.33 = (s32[]{:T(128)}, f32[8,1280]{1,0:T(8,128)S(1)}, bf16[8,640]{1,0:T(8,128)(2,1)S(1)}, bf16[64,8,320]{2,1,0:T(8,128)(2,1)}, bf16[64,8,640]{2,1,0:T(8,12...) while((s32[]{:T(128)}, f32[8,1280]{1,0:T(8,128)S(1)}, ...), condition=%wide.region_7.8_spmd, body=%wide.region_4.7_spmd.sunk | while | flops 78909440 | bytes 12079797 | solution.py:46
  3605.0 26.5 all-reduce.5.cloned.1.call-done
  3660.1 26.5 all-reduce.5.cloned.1.call-done
  3715.2 26.5 all-reduce.5.cloned.1.call-done
  3770.3 26.5 all-reduce.5.cloned.1.call-done
  3825.4 26.5 all-reduce.5.cloned.1.call-done
  3880.6 26.5 all-reduce.5.cloned.1.call-done
  3935.7 26.5 all-reduce.5.cloned.1.call-done
  3990.8 26.5 all-reduce.5.cloned.1.call-done
  4045.9 26.5 all-reduce.5.cloned.1.call-done
  4101.0 26.5 all-reduce.5.cloned.1.call-done
  4156.1 26.5 all-reduce.5.cloned.1.call-done
  4211.2 26.5 all-reduce.5.cloned.1.call-done
  4266.4 26.5 all-reduce.5.cloned.1.call-done
  4321.5 26.5 all-reduce.5.cloned.1.call-done
  4376.6 26.5 all-reduce.5.cloned.1.call-done
  4431.7 26.5 all-reduce.5.cloned.1.call-done
  4486.8 26.5 all-reduce.5.cloned.1.call-done
  4541.9 26.5 all-reduce.5.cloned.1.call-done
  4597.0 26.5 all-reduce.5.cloned.1.call-done
  4652.2 26.5 all-reduce.5.cloned.1.call-done
  4707.3 26.5 all-reduce.5.cloned.1.call-done
  4762.4 26.5 all-reduce.5.cloned.1.call-done
  4817.5 26.5 all-reduce.5.cloned.1.call-done
  4872.6 26.5 all-reduce.5.cloned.1.call-done
  4927.7 26.5 all-reduce.5.cloned.1.call-done
  4982.9 26.5 all-reduce.5.cloned.1.call-done
  5038.0 26.5 all-reduce.5.cloned.1.call-done
  5093.1 26.5 all-reduce.5.cloned.1.call-done
  5148.2 26.5 all-reduce.5.cloned.1.call-done
  5203.3 26.5 all-reduce.5.cloned.1.call-done
  5258.4 26.5 all-reduce.5.cloned.1.call-done
  5313.5 26.5 all-reduce.5.cloned.1.call-done
  5368.7 26.5 all-reduce.5.cloned.1.call-done
  5423.8 26.5 all-reduce.5.cloned.1.call-done
  5478.9 26.5 all-reduce.5.cloned.1.call-done
  5534.0 26.5 all-reduce.5.cloned.1.call-done
  5589.1 26.5 all-reduce.5.cloned.1.call-done
  5644.2 26.5 all-reduce.5.cloned.1.call-done
  5699.3 26.5 all-reduce.5.cloned.1.call-done
  5754.5 26.5 all-reduce.5.cloned.1.call-done
  5809.6 26.5 all-reduce.5.cloned.1.call-done
  5864.7 26.5 all-reduce.5.cloned.1.call-done
  5919.8 26.5 all-reduce.5.cloned.1.call-done
  5974.9 26.5 all-reduce.5.cloned.1.call-done
  6030.0 26.5 all-reduce.5.cloned.1.call-done
  6085.1 26.5 all-reduce.5.cloned.1.call-done
  6140.3 26.5 all-reduce.5.cloned.1.call-done
  6195.4 26.5 all-reduce.5.cloned.1.call-done
  6250.5 26.5 all-reduce.5.cloned.1.call-done
  6305.6 26.5 all-reduce.5.cloned.1.call-done
  6360.7 26.5 all-reduce.5.cloned.1.call-done
  6415.8 26.5 all-reduce.5.cloned.1.call-done
  6470.9 26.5 all-reduce.5.cloned.1.call-done
  6526.1 26.5 all-reduce.5.cloned.1.call-done
  6581.2 26.5 all-reduce.5.cloned.1.call-done
  6636.3 26.5 all-reduce.5.cloned.1.call-done
  6691.4 26.5 all-reduce.5.cloned.1.call-done
  6746.5 26.5 all-reduce.5.cloned.1.call-done
  6801.6 26.5 all-reduce.5.cloned.1.call-done
  6856.8 26.5 all-reduce.5.cloned.1.call-done
  6911.9 26.5 all-reduce.5.cloned.1.call-done
  6967.0 26.5 all-reduce.5.cloned.1.call-done
  (1936 shorter events, 5420.2 us)
Async XLA Ops:
  3545.4 30.9 all-reduce.5.cloned.1.call-start
  3600.6 30.9 all-reduce.5.cloned.1.call-start
  3655.7 30.9 all-reduce.5.cloned.1.call-start
  3710.8 30.9 all-reduce.5.cloned.1.call-start
  3765.9 30.9 all-reduce.5.cloned.1.call-start
  3821.0 30.9 all-reduce.5.cloned.1.call-start
  3876.2 30.9 all-reduce.5.cloned.1.call-start
  3931.3 30.9 all-reduce.5.cloned.1.call-start
  3986.4 30.9 all-reduce.5.cloned.1.call-start
  4041.5 30.9 all-reduce.5.cloned.1.call-start
  4096.6 30.9 all-reduce.5.cloned.1.call-start
  4151.7 30.9 all-reduce.5.cloned.1.call-start
  4206.8 30.9 all-reduce.5.cloned.1.call-start
  4262.0 30.9 all-reduce.5.cloned.1.call-start
  4317.1 30.9 all-reduce.5.cloned.1.call-start
  4372.2 30.9 all-reduce.5.cloned.1.call-start
  4427.3 30.9 all-reduce.5.cloned.1.call-start
  4482.4 30.9 all-reduce.5.cloned.1.call-start
  4537.5 30.9 all-reduce.5.cloned.1.call-start
  4592.6 30.9 all-reduce.5.cloned.1.call-start
  4647.8 30.9 all-reduce.5.cloned.1.call-start
  4702.9 30.9 all-reduce.5.cloned.1.call-start
  4758.0 30.9 all-reduce.5.cloned.1.call-start
  4813.1 30.9 all-reduce.5.cloned.1.call-start
  4868.2 30.9 all-reduce.5.cloned.1.call-start
  4923.3 30.9 all-reduce.5.cloned.1.call-start
  4978.5 30.9 all-reduce.5.cloned.1.call-start
  5033.6 30.9 all-reduce.5.cloned.1.call-start
  5088.7 30.9 all-reduce.5.cloned.1.call-start
  5143.8 30.9 all-reduce.5.cloned.1.call-start
  5198.9 30.9 all-reduce.5.cloned.1.call-start
  5254.0 30.9 all-reduce.5.cloned.1.call-start
  5309.1 30.9 all-reduce.5.cloned.1.call-start
  5364.3 30.9 all-reduce.5.cloned.1.call-start
  5419.4 30.9 all-reduce.5.cloned.1.call-start
  5474.5 30.9 all-reduce.5.cloned.1.call-start
  5529.6 30.9 all-reduce.5.cloned.1.call-start
  5584.7 30.9 all-reduce.5.cloned.1.call-start
  5639.8 30.9 all-reduce.5.cloned.1.call-start
  5694.9 30.9 all-reduce.5.cloned.1.call-start
  5750.1 30.9 all-reduce.5.cloned.1.call-start
  5805.2 30.9 all-reduce.5.cloned.1.call-start
  5860.3 30.9 all-reduce.5.cloned.1.call-start
  5915.4 30.9 all-reduce.5.cloned.1.call-start
  5970.5 30.9 all-reduce.5.cloned.1.call-start
  6025.6 30.9 all-reduce.5.cloned.1.call-start
  6080.7 30.9 all-reduce.5.cloned.1.call-start
  6135.9 30.9 all-reduce.5.cloned.1.call-start
  6191.0 30.9 all-reduce.5.cloned.1.call-start
  6246.1 30.9 all-reduce.5.cloned.1.call-start
  6301.2 30.9 all-reduce.5.cloned.1.call-start
  6356.3 30.9 all-reduce.5.cloned.1.call-start
  6411.4 30.9 all-reduce.5.cloned.1.call-start
  6466.6 30.9 all-reduce.5.cloned.1.call-start
  6521.7 30.9 all-reduce.5.cloned.1.call-start
  6576.8 30.9 all-reduce.5.cloned.1.call-start
  6631.9 30.9 all-reduce.5.cloned.1.call-start
  6687.0 30.9 all-reduce.5.cloned.1.call-start
  6742.1 30.9 all-reduce.5.cloned.1.call-start
  6797.2 30.9 all-reduce.5.cloned.1.call-start
  6852.4 30.9 all-reduce.5.cloned.1.call-start
  6907.5 30.9 all-reduce.5.cloned.1.call-start
  6962.6 30.9 all-reduce.5.cloned.1.call-start
  7017.7 30.9 all-reduce.5.cloned.1.call-start
  (66 other events, 1981.7 us)
Sparse Core Ops, SparseCore 0:
  80.2 26.3 all-reduce.2
  3605.1 26.3 all-reduce.4
  3660.2 26.3 all-reduce.4
  3715.3 26.3 all-reduce.4
  3770.4 26.3 all-reduce.4
  3825.6 26.3 all-reduce.4
  3880.7 26.3 all-reduce.4
  3935.8 26.3 all-reduce.4
  3990.9 26.3 all-reduce.4
  4046.0 26.3 all-reduce.4
  4101.1 26.3 all-reduce.4
  4156.3 26.3 all-reduce.4
  4211.4 26.3 all-reduce.4
  4266.5 26.3 all-reduce.4
  4321.6 26.3 all-reduce.4
  4376.7 26.3 all-reduce.4
  4431.8 26.3 all-reduce.4
  4486.9 26.3 all-reduce.4
  4542.1 26.3 all-reduce.4
  4597.2 26.3 all-reduce.4
  4652.3 26.3 all-reduce.4
  4707.4 26.3 all-reduce.4
  4762.5 26.3 all-reduce.4
  4817.6 26.3 all-reduce.4
  4872.7 26.3 all-reduce.4
  4927.9 26.3 all-reduce.4
  4983.0 26.3 all-reduce.4
  5038.1 26.3 all-reduce.4
  5093.2 26.3 all-reduce.4
  5148.3 26.3 all-reduce.4
  5203.4 26.3 all-reduce.4
  5258.5 26.3 all-reduce.4
  5313.7 26.3 all-reduce.4
  5368.8 26.3 all-reduce.4
  5423.9 26.3 all-reduce.4
  5479.0 26.3 all-reduce.4
  5534.1 26.3 all-reduce.4
  5589.2 26.3 all-reduce.4
  5644.3 26.3 all-reduce.4
  5699.5 26.3 all-reduce.4
  5754.6 26.3 all-reduce.4
  5809.7 26.3 all-reduce.4
  5864.8 26.3 all-reduce.4
  5919.9 26.3 all-reduce.4
  5975.0 26.3 all-reduce.4
  6030.2 26.3 all-reduce.4
  6085.3 26.3 all-reduce.4
  6140.4 26.3 all-reduce.4
  6195.5 26.3 all-reduce.4
  6250.6 26.3 all-reduce.4
  6305.7 26.3 all-reduce.4
  6360.8 26.3 all-reduce.4
  6416.0 26.3 all-reduce.4
  6471.1 26.3 all-reduce.4
  6526.2 26.3 all-reduce.4
  6581.3 26.3 all-reduce.4
  6636.4 26.3 all-reduce.4
  6691.5 26.3 all-reduce.4
  6746.6 26.3 all-reduce.4
  6801.8 26.3 all-reduce.4
  6856.9 26.3 all-reduce.4
  6912.0 26.3 all-reduce.4
  6967.1 26.3 all-reduce.4
  7022.2 26.3 all-reduce.4
  (64 shorter events, 1681.6 us)
where the time goes:
time: 7100 us; the launch traced here: 7080 us
  waiting for transfers between devices  3390 us (48%)
  blocking collectives  2570 us (36%)
  matrix products  698 us (10%)
  other arithmetic  311 us (4%)
  local copies, waits for them, and re-layouts  86.5 us (1%)
    psum x128, waiting for transfers between devices, gru_step(): gate_pre = lax.psum(part_sum, 'row') + gate_bias  3390 us
    psum x128, blocking collectives, gru_step(): lax.psum(jnp.dot(gated_row, w_hn, preferred_element_type=jnp.float32), 'r...  1420 us
    all_gather x256, blocking collectives, gather_rows(): gathered = lax.all_gather(col_part, 'col', axis=1, tiled=True)  1140 us
    dot_general x128, matrix products, gru_step(): jnp.einsum('bk,kgn->bgn', step_in, w_x, preferred_element_type=jnp.float32)  404 us
    dot_general x128, matrix products, gru_step(): jnp.dot(gated_row, w_hn, preferred_element_type=jnp.float32)  224 us
  transfers between devices with their start and end apart: 128, of which 128 were waited for; matrix products, arithmetic and copies ran while one was open for 0% of the time, Pallas kernels for 0%

commit v1 on v0

v1 whole, which is shorter than its diff:
```python
import functools

import jax
import jax.numpy as jnp
from jax import lax
from jax.experimental import pallas as pl
from jax.experimental.pallas import tpu as pltpu
from jax.sharding import PartitionSpec as P

MESH = pl.DeviceIdType.MESH
F32 = jnp.float32
BF16 = jnp.bfloat16

STEPS = 64
BATCH = 8
HALF = 1280
ROWS = 640
PART = 640
OWN = 320
CHUNK = 8
CHUNKS = STEPS // CHUNK
RING = 4


def gru_kernel(w_in, wx_in, p_in, h0, bias, seq_out, fin_out,
               w, pbuf, hid, rhb, state, outbuf, oscr, finsrc, finbuf,
               w_send, w_recv, wx_send, wx_recv, p_send, p_recv, h_send, h_recv,
               n_send, r_send, r_recv, o_send, o_recv, f_send, f_recv):
    row = lax.axis_index("row")
    col = lax.axis_index("col")
    chip = row // 2
    core = row % 2
    other = 1 - core
    hub = chip == col
    layer = chip

    def device(r, c):
        return {"row": r, "col": c}

    def remote(src, dst, send, recv, r, c):
        return pltpu.make_async_remote_copy(
            src_ref=src, dst_ref=dst, send_sem=send, recv_sem=recv,
            device_id=device(r, c), device_id_type=MESH)

    def arrived(ref, sem):
        pltpu.make_async_copy(ref, ref, sem).wait()

    def p_copy(k):
        at = pl.ds(k * CHUNK, CHUNK)
        return p_in.at[at], pbuf.at[chip, core, at], p_send.at[k], p_recv.at[k, chip, core], col, 0

    slot = jnp.where(hub, 0, 1)
    my_rows = pl.ds(core * ROWS, ROWS)

    def w_copy(l):
        return w_in.at[l], w.at[slot, my_rows], w_send.at[l], w_recv.at[slot, core], 2 * l + col, l

    def wx_copy(half):
        return (wx_in.at[half], w.at[chip, my_rows, pl.ds(0, 3 * PART)], wx_send.at[half],
                wx_recv.at[row], 2 * (1 - col) + half, col)

    def start(spec):
        src, dst, send, recv, r, c = spec
        here = (r == row) & (c == col)

        @pl.when(here)
        def _():
            pltpu.make_async_copy(src, dst, recv).start()

        @pl.when(jnp.logical_not(here))
        def _():
            remote(src, dst, send, recv, r, c).start()

    def finish(spec):
        src, dst, send, recv, r, c = spec
        here = (r == row) & (c == col)

        @pl.when(jnp.logical_not(here))
        def _():
            remote(src, dst, send, recv, r, c).wait_send()

    start(p_copy(0))
    start(w_copy(0))
    start(w_copy(1))
    for half in range(2):
        start(wx_copy(half))
    for k in range(1, CHUNKS):
        start(p_copy(k))

    @pl.when(hub)
    def _():
        first = layer == 0
        for b in range(2):
            hid[0, b] = h0[layer, :, b * HALF:(b + 1) * HALF].astype(BF16)
        state[...] = h0[layer, :, pl.ds(pl.multiple_of(core * HALF, HALF), HALF)]

        @pl.when(jnp.logical_not(first))
        def _():
            def clear(t, carry):
                for b in range(2):
                    pbuf[1, b, t] = jnp.zeros((BATCH, 3 * PART), F32)
                return carry
            lax.fori_loop(0, STEPS, clear, 0)

        for s in range(2):
            for b in range(2):
                arrived(w.at[s, pl.ds(b * ROWS, ROWS)], w_recv.at[s, b])

        def partner(t):
            return remote(hid.at[t, core], hid.at[t, core], n_send.at[t % RING], h_recv.at[t, core],
                          2 * chip + other, col)

        def helper(t, y, b):
            return remote(hid.at[t, core], hid.at[t, core], h_send.at[t % RING, y, b], h_recv.at[t, core],
                          2 * (1 - y) + b, y)

        def piece(i, k):
            at = pl.ds(k * CHUNK, CHUNK)
            return remote(outbuf.at[i, at], oscr.at[at], o_send.at[i, k], o_recv.at[k], i, core)

        def mine(i):
            return (row == i) & (col == core)

        def gate(t, g):
            cols = pl.ds(g * PART, PART)
            return jnp.concatenate(
                [pbuf[0, b, t, :, cols] + pbuf[1, b, t, :, cols] for b in range(2)], axis=1)

        def tick(t, carry):
            @pl.when(first & (t % CHUNK == 0))
            def _():
                k = t // CHUNK
                at = pl.ds(k * CHUNK, CHUNK)
                for a in range(2):
                    for b in range(2):
                        arrived(pbuf.at[a, b, at], p_recv.at[k, a, b])

            @pl.when(jnp.logical_not(first))
            def _():
                for b in range(2):
                    arrived(pbuf.at[0, b, t], p_recv.at[t, 0, b])

            ru_own = jnp.dot(hid[t, core], w[0, :, 0:2 * HALF], preferred_element_type=F32)

            @pl.when(t > 0)
            def _():
                partner(t).wait_send()
                arrived(hid.at[t, other], h_recv.at[t, other])

            r_sum = ru_own[:, 0:HALF] + jnp.dot(hid[t, other], w[1, :, 0:HALF], preferred_element_type=F32)
            reset = jax.nn.sigmoid(gate(t, 0) + r_sum)
            q = t % 2
            rhb[q, core] = (reset * state[...]).astype(BF16)
            swap = remote(rhb.at[q, core], rhb.at[q, core], r_send.at[q], r_recv.at[q], 2 * chip + other, col)
            swap.start()
            u_sum = ru_own[:, HALF:] + jnp.dot(hid[t, other], w[1, :, HALF:2 * HALF], preferred_element_type=F32)
            update = jax.nn.sigmoid(gate(t, 1) + u_sum)
            n_sum = gate(t, 2) + jnp.dot(rhb[q, core], w[0, :, 2 * HALF:], preferred_element_type=F32)
            swap.wait_send()
            arrived(rhb.at[q, other], r_recv.at[q])
            n_sum = n_sum + jnp.dot(rhb[q, other], w[1, :, 2 * HALF:], preferred_element_type=F32)
            cand = jnp.tanh(n_sum)
            h_next = (1.0 - update) * cand + update * state[...]
            state[...] = h_next
            h_bf = h_next.astype(BF16)
            hid[t + 1, core] = h_bf

            @pl.when(t < STEPS - 1)
            def _():
                partner(t + 1).start()

            @pl.when(first)
            def _():
                for y in range(2):
                    for b in range(2):
                        @pl.when(t >= RING)
                        def _():
                            helper(t + 1 - RING, y, b).wait_send()
                        helper(t + 1, y, b).start()

            @pl.when(jnp.logical_not(first))
            def _():
                for i in range(4):
                    outbuf[i, t] = h_bf[:, i * OWN:(i + 1) * OWN]

                @pl.when(t % CHUNK == CHUNK - 1)
                def _():
                    for i in range(4):
                        @pl.when(jnp.logical_not(mine(i)))
                        def _():
                            piece(i, t // CHUNK).start()
            return carry

        lax.fori_loop(0, STEPS, tick, 0)

        last = state[...]
        for i in range(4):
            finsrc[i] = last[:, i * OWN:(i + 1) * OWN]

        def fin_copy(i):
            return remote(finsrc.at[i], finbuf.at[layer], f_send.at[i], f_recv.at[layer], i, core)

        for i in range(4):
            @pl.when(mine(i))
            def _():
                finbuf[layer] = finsrc[i]

                @pl.when(jnp.logical_not(first))
                def _():
                    def take(t, carry):
                        oscr[t] = outbuf[i, t]
                        return carry
                    lax.fori_loop(0, STEPS, take, 0)

            @pl.when(jnp.logical_not(mine(i)))
            def _():
                fin_copy(i).start()

        for i in range(4):
            @pl.when(jnp.logical_not(mine(i)))
            def _():
                fin_copy(i).wait_send()

                @pl.when(jnp.logical_not(first))
                def _():
                    for k in range(CHUNKS):
                        piece(i, k).wait_send()

        @pl.when(first)
        def _():
            for t in range(STEPS + 1 - RING, STEPS + 1):
                for y in range(2):
                    for b in range(2):
                        helper(t, y, b).wait_send()

    @pl.when(jnp.logical_not(hub))
    def _():
        for i in range(4):
            arrived(w.at[i // 2, pl.ds((i % 2) * ROWS, ROWS), pl.ds(0, 3 * PART)], wx_recv.at[i])

        def project(t):
            return remote(pbuf.at[0, core, t], pbuf.at[0, core, t], h_send.at[t % RING, 0, 0],
                          p_recv.at[t, 0, core], 2 + col, 1)

        def tick(t, carry):
            for b in range(2):
                arrived(hid.at[t + 1, b], h_recv.at[t + 1, b])
            total = jnp.dot(hid[t + 1, 0], w[0, :, 0:3 * PART], preferred_element_type=F32)
            total = total + jnp.dot(hid[t + 1, 1], w[1, :, 0:3 * PART], preferred_element_type=F32)
            pbuf[0, core, t] = total + bias[...]

            @pl.when(t >= RING)
            def _():
                project(t - RING).wait_send()
            project(t).start()
            return carry

        lax.fori_loop(0, STEPS, tick, 0)
        for t in range(STEPS - RING, STEPS):
            project(t).wait_send()

    for l in range(2):
        finish(w_copy(l))
        finish(wx_copy(l))
    for k in range(CHUNKS):
        finish(p_copy(k))
    for l in range(2):
        @pl.when(jnp.logical_not((row == 2 * l + col) & (col == l)))
        def _():
            arrived(finbuf.at[l], f_recv.at[l])

    @pl.when(jnp.logical_not((row == 2 + col) & (col == 1)))
    def _():
        for k in range(CHUNKS):
            at = pl.ds(k * CHUNK, CHUNK)
            arrived(oscr.at[at], o_recv.at[k])

    def emit(t, carry):
        seq_out[t] = oscr[t]
        return carry
    lax.fori_loop(0, STEPS, emit, 0)
    fin_out[...] = finbuf[...]


def gru_call(w_in, wx_in, p_in, h0, bias):
    dma = pltpu.SemaphoreType.DMA
    any_spec = pl.BlockSpec(memory_space=pl.ANY)
    vmem_spec = pl.BlockSpec(memory_space=pltpu.VMEM)
    return pl.pallas_call(
        gru_kernel,
        out_shape=(jax.ShapeDtypeStruct((STEPS, BATCH, OWN), BF16), jax.ShapeDtypeStruct((2, BATCH, OWN), F32)),
        in_specs=[any_spec, any_spec, any_spec, vmem_spec, vmem_spec],
        out_specs=(vmem_spec, vmem_spec),
        scratch_shapes=[
            pltpu.VMEM((2, HALF, 3 * HALF), BF16),
            pltpu.VMEM((2, 2, STEPS, BATCH, 3 * PART), F32),
            pltpu.VMEM((STEPS + 1, 2, BATCH, HALF), BF16),
            pltpu.VMEM((2, 2, BATCH, HALF), BF16),
            pltpu.VMEM((BATCH, HALF), F32),
            pltpu.VMEM((4, STEPS, BATCH, OWN), BF16),
            pltpu.VMEM((STEPS, BATCH, OWN), BF16),
            pltpu.VMEM((4, BATCH, OWN), F32),
            pltpu.VMEM((2, BATCH, OWN), F32),
            dma((2,)), dma((2, 2)),
            dma((2,)), dma((4,)),
            dma((CHUNKS,)), dma((STEPS, 2, 2)),
            dma((RING, 2, 2)), dma((STEPS + 1, 2)),
            dma((RING,)), dma((2,)), dma((2,)),
            dma((4, CHUNKS)), dma((CHUNKS,)),
            dma((4,)), dma((2,)),
        ],
        compiler_params=pltpu.CompilerParams(has_side_effects=True, vmem_limit_bytes=62 * 2**20),
        name="gru",
    )(w_in, wx_in, p_in, h0, bias)


def solution(mesh):
    seq_spec = P(None, "data", "row")
    out_spec = P(None, "data", ("col", "row"))
    wide_spec = P("row", None, "col")
    square_spec = P("row", "col")
    bias_spec = P(None, "col")
    swap = [(0, 1), (1, 0), (2, 3), (3, 2)]

    def halves(w):
        return w.reshape(ROWS, 3, 2, PART).transpose(2, 0, 1, 3).reshape(2, ROWS, 3 * PART)

    def device_body(x_rows, h_rows, wx_l1, whru_l1, whn_l1, bias_l1, wx_l2, whru_l2, whn_l2, bias_l2):
        row = lax.axis_index("row")
        core = row % 2
        chip = row // 2

        def bias_half(b):
            return lax.dynamic_index_in_dim(b.reshape(3, 2, PART), core, 1, keepdims=False).reshape(1, 3 * PART)

        wx1 = halves(wx_l1)
        own = lax.dynamic_index_in_dim(wx1, core, 0, keepdims=False)
        theirs = lax.ppermute(lax.dynamic_index_in_dim(wx1, 1 - core, 0, keepdims=False), "row", swap)
        x_own = x_rows.reshape(STEPS * BATCH, ROWS)
        x_theirs = lax.ppermute(x_own, "row", swap)
        p1 = jnp.dot(x_own, own, preferred_element_type=F32) + jnp.dot(x_theirs, theirs, preferred_element_type=F32)
        p1 = p1 + jnp.where(chip == 0, bias_half(bias_l1), 0.0)
        p1 = p1.reshape(STEPS, BATCH, 3 * PART)

        h0 = lax.all_gather(h_rows, "row", axis=2, tiled=True)
        w_rec = jnp.stack([
            jnp.concatenate([whru_l1.reshape(ROWS, 2 * HALF), whn_l1], axis=1),
            jnp.concatenate([whru_l2.reshape(ROWS, 2 * HALF), whn_l2], axis=1)])
        return gru_call(w_rec, halves(wx_l2), p1, h0, bias_half(bias_l2))

    return jax.shard_map(
        device_body,
        mesh=mesh,
        in_specs=(seq_spec, seq_spec, wide_spec, wide_spec, square_spec, bias_spec, wide_spec, wide_spec, square_spec, bias_spec),
        out_specs=(out_spec, out_spec),
        check_vma=False,
    )
```

time: 7100 us -> 632 us (0.09)
  waiting for transfers between devices: 3390 us -> 0.01 us
  blocking collectives: 2570 us -> 10 us
  matrix products: 698 us -> 12.5 us
  Pallas kernels: 0 us -> 547 us
  other arithmetic: 311 us -> 12.5 us
    psum x128 -> x0, waiting for transfers between devices: 3390 us -> none  [gru_step(): gate_pre = lax.psum(part_sum, 'row') + gate_bias]
    psum x128 -> x0, blocking collectives: 1420 us -> none  [gru_step(): lax.psum(jnp.dot(gated_row, w_hn, preferred_element_type=jnp.float32), 'r...]
    all_gather x257 -> x1, blocking collectives: 1150 us -> 10 us  [device_body(): h0 = lax.all_gather(h_rows, 'row', axis=2, tiled=True)]
    dot_general x384 -> x2, matrix products: 698 us -> 12.5 us  [the longest x1 6.74 us: device_body(): jnp.dot(x_theirs, theirs, preferred_element_type=F32)]
    pallas_call x0 -> x1, Pallas kernels: none -> 547 us  [gru_call(): pl.pallas_call(gru_kernel, out_shape=(jax.ShapeDtypeStruct((STEPS, BATCH,...]
    add x128 -> x0, other arithmetic: 117 us -> none  [gru_step(): gate_pre = lax.psum(part_sum, 'row') + gate_bias]
    convert_element_type x257 -> x0, other arithmetic: 108 us -> none  [the longest x128 105 us: gru_step(): next_row = gather_rows(h_next.astype(jnp.bfloat16), row_idx, row_block)]
    concatenate x128 -> x0, other arithmetic: 85.1 us -> none  [gru_step(): jnp.concatenate([in_part[:, :2] + rec_part, in_part[:, 2:]], axis=1)]
  transfers between devices with their start and end apart: 128 -> 2, of which waited for: 128 -> 0; matrix products, arithmetic and copies ran while one was open for 0% -> 7% of each run, Pallas kernels for 0% -> 0%
where the time goes in v1:
time: 632 us; the launch traced here: 631 us
  Pallas kernels  547 us (87%)
  local copies, waits for them, and re-layouts  48.1 us (8%)
  other arithmetic  12.5 us (2%)
  matrix products  12.5 us (2%)
  blocking collectives  10 us (2%)
    pallas_call x1, Pallas kernels, gru_call(): pl.pallas_call(gru_kernel, out_shape=(jax.ShapeDtypeStruct((STEPS, BATCH,...  547 us
    unnamed x22, local copies, waits for them, and re-layouts  26.8 us
  transfers between devices with their start and end apart: 2, of which 0 were waited for; matrix products, arithmetic and copies ran while one was open for 7% of the time, Pallas kernels for 0%

profile of v1, /device:TPU:0, one launch (start us, length us, event | category | flops | bytes accessed | tf_op | source)
XLA Modules:
  0.0 631.5 jit_solution(16484831833248239238)
XLA Ops:
  0.6 0.0 copy-start
  0.7 8.2 %copy.18 = bf16[640,3,1280]{0,2,1:T(8,128)(2,1)} copy(bf16[640,3,1280]{2,0,1:T(8,128)(2,1)} %param.12) | data formatting | bytes 9830400 | tf_op args[2]
  8.9 5.0 copy.19
  13.8 0.0 copy-start.6
  13.8 3.3 dynamic-slice_bitcast_fusion
  17.2 0.9 collective-permute-start
  18.0 0.0 collective-permute-start.1
  18.1 0.0 copy-done.6
  18.1 0.0 copy-done
  18.2 0.6 copy.24
  18.8 2.5 copy.22
  21.2 4.2 copy.23
  25.4 8.2 %copy.16 = bf16[640,3,1280]{0,2,1:T(8,128)(2,1)} copy(bf16[640,3,1280]{2,0,1:T(8,128)(2,1)} %param.16) | data formatting | bytes 9830400 | tf_op args[6]
  33.6 5.0 copy.17
  38.6 0.0 copy-start.5
  38.6 7.9 %copy.21.wx_in = bf16[2,640,1920]{2,1,0:T(8,128)(2,1)} copy(bf16[2,640,1920]{1,2,0:T(8,128)(2,1)} %bitcast.36) | data formatting | bytes 9830400 | tf_op jit(solution)/shard_map/reshape | solution.py:326
  46.6 0.0 copy-done.5
  46.6 10.0 %all_gather.3.h0 = f32[2,8,2560]{2,1,0:T(8,128)} all-gather(f32[2,8,640]{2,1,0:T(8,128)S(1)} %copy-done.5), channel_id=1, replica_groups=mesh['data'=1,'col'=2,'row'=4] {'row'}, dimensions={2}, use_global_device_ids=true | all-gather | bytes 204800 | tf_op jit(solution)/shard_map/all_gather | solution.py:345
  56.6 0.0 copy-start.2
  56.6 0.0 copy-start.3
  56.6 0.0 copy-start.4
  56.6 5.7 fusion
  62.3 0.0 copy-done.2
  62.3 0.0 copy-done.3
  62.3 0.0 copy-done.4
  62.3 3.9 maximum_bitcast_fusion
  66.2 8.6 %pad_maximum_fusion.w_in = bf16[2,640,3840]{2,1,0:T(8,128)(2,1)} fusion(bf16[1,640,3840]{2,1,0:T(8,128)(2,1)} %get-tuple-element.3, bf16[1,640,3840]{2,1,0:T(8,128)(2,1)} %get-tuple-element.2), kind=kLoop, calls=%fused_computation | loop fusion | flops 4915200 | bytes 19660800 | tf_op jit(solution)/shard_map/stack | solution.py:346
  74.8 0.0 collective-permute-done.1
  74.8 0.0 collective-permute-done
  74.8 6.7 %add_bitcast_fusion.p_in = f32[64,8,1920]{2,1,0:T(8,128)} fusion(f32[1920,512]{0,1:T(8,128)} %fusion, bf16[640,1920]{0,1:T(8,128)(2,1)} %collective-permute-done, bf16[512,640]{1,0:T(8,128)(2,1)} %collective-permute-done.1, f32[1920]{0:T(1024)S(1)} %select_n.43), kind=kOutput, calls=%fused_computation.3 | convolution fusion | flops 1260257280 | bytes 10984960 | tf_op jit(solution)/shard_map/dot_general | solution.py:341
  81.5 0.0 copy-start.1
  81.5 546.8 %gru.1 = (bf16[64,8,320]{2,1,0:T(8,128)(2,1)}, f32[2,8,320]{2,1,0:T(8,128)}) custom-call(bf16[2,640,3840]{2,1,0:T(8,128)(2,1)} %pad_maximum_fusion.w_in, bf16[2,640,1920]{2,1,0:T(8,128)(2,1)} %copy.21.wx_in, f32[64,8,1920]{2,1,0:T(8,128)} %add_bitcast_fusion.p_in, f32[2,8,2560]{2,1,0:T(8,128)} %all_gather.3.h0, f32[1,1920]{1,0:T(1,128)} %bitcast.45), custom_call_target="tpu_custom_call" | custom-call | tf_op jit(solution)/shard_map/gru/pallas_call | solution.py:289
  628.3 1.8 copy.27
  630.1 1.3 copy.28
  631.4 0.0 copy-done.1
  (4 shorter events, 0.1 us)
Async XLA Ops:
  0.6 17.5 %copy-start = (f32[3,1280]{1,0:T(4,128)S(1)}, f32[3,1280]{1,0:T(4,128)}, u32[]{:S(2)}) copy-start(f32[3,1280]{1,0:T(4,128)} %param.19) | copy-start | bytes 46084
  13.8 4.2 copy-start.6
  17.2 57.6 %collective-permute-start = (bf16[640,1920]{0,1:T(8,128)(2,1)}, bf16[640,1920]{0,1:T(8,128)(2,1)}, u32[]{:S(2)}, u32[]{:S(2)}) collective-permute-start(bf16[640,1920]{0,1:T(8,128)(2,1)} %dynamic-slice_bitcast_fusion), channel_id=1, source_target_pairs={{0,1},{1,0},{2,3},{3,2},{4,5},{5,4},{6,7},{7,6}} | collective-permute-start | bytes 7372808 | tf_op jit(solution)/shard_map/ppermute | solution.py:338
  18.0 56.8 %collective-permute-start.1 = (bf16[512,640]{1,0:T(8,128)(2,1)}, bf16[512,640]{1,0:T(8,128)(2,1)}, u32[]{:S(2)}, u32[]{:S(2)}) collective-permute-start(bf16[512,640]{1,0:T(8,128)(2,1)} %bitcast.9), channel_id=1, source_target_pairs={{0,1},{1,0},{2,3},{3,2},{4,5},{5,4},{6,7},{7,6}} | collective-permute-start | bytes 1966088 | tf_op jit(solution)/shard_map/ppermute | solution.py:340
  38.6 7.9 %copy-start.5 = (f32[2,8,640]{2,1,0:T(8,128)S(1)}, f32[2,8,640]{2,1,0:T(8,128)}, u32[]{:S(2)}) copy-start(f32[2,8,640]{2,1,0:T(8,128)} %param.11) | copy-start | bytes 122884
  56.6 5.8 copy-start.2
  56.6 5.8 copy-start.3
  56.6 5.8 copy-start.4
  81.5 549.9 %copy-start.1 = (f32[3,1280]{1,0:T(4,128)S(1)}, f32[3,1280]{1,0:T(4,128)}, u32[]{:S(2)}) copy-start(f32[3,1280]{1,0:T(4,128)} %param.19) | copy-start | bytes 46084

commit v2 on v1

--- a/solution.py
+++ b/solution.py
@@ -22,8 +22,9 @@
 RING = 4
 
 
-def gru_kernel(w_in, wx_in, p_in, h0, bias, seq_out, fin_out,
-               w, pbuf, hid, rhb, state, outbuf, oscr, finsrc, finbuf,
+def gru_kernel(x_in, wx1_in, wx2_in, ru1_in, ru2_in, n1_in, n2_in, h_in, bias1, bias2, seq_out, fin_out,
+               w, pbuf, psrc, xs, wx1, h0, hid, rhb, state, outbuf, oscr, finsrc, finbuf,
+               x_send, x_recv, v_send, v_recv, z_send, z_recv, s_send, s_recv, t_send,
                w_send, w_recv, wx_send, wx_recv, p_send, p_recv, h_send, h_recv,
                n_send, r_send, r_recv, o_send, o_recv, f_send, f_recv):
     row = lax.axis_index("row")
@@ -45,20 +46,6 @@
     def arrived(ref, sem):
         pltpu.make_async_copy(ref, ref, sem).wait()
 
-    def p_copy(k):
-        at = pl.ds(k * CHUNK, CHUNK)
-        return p_in.at[at], pbuf.at[chip, core, at], p_send.at[k], p_recv.at[k, chip, core], col, 0
-
-    slot = jnp.where(hub, 0, 1)
-    my_rows = pl.ds(core * ROWS, ROWS)
-
-    def w_copy(l):
-        return w_in.at[l], w.at[slot, my_rows], w_send.at[l], w_recv.at[slot, core], 2 * l + col, l
-
-    def wx_copy(half):
-        return (wx_in.at[half], w.at[chip, my_rows, pl.ds(0, 3 * PART)], wx_send.at[half],
-                wx_recv.at[row], 2 * (1 - col) + half, col)
-
     def start(spec):
         src, dst, send, recv, r, c = spec
         here = (r == row) & (c == col)
@@ -79,20 +66,136 @@
         def _():
             remote(src, dst, send, recv, r, c).wait_send()
 
+    slot = jnp.where(hub, 0, 1)
+    my_rows = pl.ds(core * ROWS, ROWS)
+    my_cols = pl.ds(pl.multiple_of(core * ROWS, ROWS), ROWS)
+
+    def gate_cols(g):
+        return pl.ds(g * HALF, HALF)
+
+    def weight(l, g):
+        return (n1_in, n2_in)[l] if g == 2 else (ru1_in, ru2_in)[l].at[g]
+
+    def x_copy(to):
+        return x_in, xs.at[:, my_cols], x_send.at[0], x_recv.at[core], 2 * chip + to, col
+
+    def wx1_copy(to, g):
+        half = pl.ds(pl.multiple_of(to * PART, PART), PART)
+        return (wx1_in.at[g, :, half], wx1.at[my_rows, pl.ds(g * PART, PART)], v_send.at[g], v_recv.at[core, g],
+                2 * chip + to, col)
+
+    def h0_copy(to):
+        return h_in.at[col], h0.at[row], z_send.at[to], z_recv.at[row], 2 * col + to, col
+
+    def w_copy(l, g):
+        return (weight(l, g), w.at[slot, my_rows, gate_cols(g)], w_send.at[l, g], w_recv.at[slot, core, g, 0],
+                2 * l + col, l)
+
+    def stage_rows(g):
+        return pl.ds(g * (ROWS // 2), ROWS // 2)
+
+    stage_cols = pl.ds(3 * PART, HALF)
+
+    def stage_copy(l, h, g):
+        src = weight(1 - l, g).at[pl.ds(h * (ROWS // 2), ROWS // 2)]
+        r, c = (2 * (1 - l) + core, l) if h == 0 else (2 * l + core, 1 - l)
+        return src, w.at[l, stage_rows(g), stage_cols], s_send.at[h, g], s_recv.at[l, g], r, c
+
+    def forward_copy(l, g):
+        h = jnp.where(col == l, 0, 1)
+        rows = pl.ds(core * ROWS + h * (ROWS // 2), ROWS // 2)
+        return (w.at[l, stage_rows(g), stage_cols], w.at[0, rows, gate_cols(g)], t_send.at[l, g],
+                w_recv.at[0, core, g, h], 2 * (1 - l) + l, 1 - l)
+
+    def wx_copy(half, g):
+        return (wx2_in.at[g, :, pl.ds(half * PART, PART)], w.at[chip, my_rows, pl.ds(g * PART, PART)],
+                wx_send.at[half, g], wx_recv.at[row, g], 2 * (1 - col) + half, col)
+
+    def p_copy(k):
+        at = pl.ds(k * CHUNK, CHUNK)
+        return psrc.at[at], pbuf.at[chip, core, at], p_send.at[k], p_recv.at[k, chip, core], col, 0
+
+    for to in (core, other):
+        start(x_copy(to))
+        for g in range(3):
+            start(wx1_copy(to, g))
+    for to in range(2):
+        start(h0_copy(to))
+    for l in range(2):
+        @pl.when(hub & (chip == l))
+        def _():
+            for g in range(3):
+                for h in range(2):
+                    start(stage_copy(l, h, g))
+            for g in range(3):
+                start(w_copy(l, g))
+
+    @pl.when(jnp.logical_not(hub))
+    def _():
+        for g in range(2):
+            for l in range(2):
+                start(w_copy(l, g))
+
+    for b in range(2):
+        arrived(xs.at[:, pl.ds(b * ROWS, ROWS)], x_recv.at[b])
+        for g in range(3):
+            arrived(wx1.at[pl.ds(b * ROWS, ROWS), pl.ds(g * PART, PART)], v_recv.at[b, g])
+
+    def bias_of(ref, g):
+        return ref[g:g + 1, my_cols]
+
+    def project_x(k, carry):
+        lines = xs[pl.ds(k * CHUNK * BATCH, CHUNK * BATCH), :]
+        for g in range(3):
+            total = jnp.dot(lines, wx1[:, g * PART:(g + 1) * PART], preferred_element_type=F32)
+            total = total + jnp.where(chip == 0, bias_of(bias1, g), 0.0)
+            psrc[pl.ds(k * CHUNK, CHUNK), :, g * PART:(g + 1) * PART] = total.reshape(CHUNK, BATCH, PART)
+        return carry
+
+    lax.fori_loop(0, CHUNKS, project_x, 0)
     start(p_copy(0))
-    start(w_copy(0))
-    start(w_copy(1))
-    for half in range(2):
-        start(wx_copy(half))
+
+    for l in range(2):
+        @pl.when(hub & (chip == l))
+        def _():
+            for g in range(3):
+                for h in range(2):
+                    finish(stage_copy(l, h, g))
+            for g in range(3):
+                for half in range(2):
+                    start(wx_copy(half, g))
+            if l == 1:
+                for g in range(3):
+                    for half in range(2):
+                        finish(wx_copy(half, g))
+
+    @pl.when(jnp.logical_not(hub))
+    def _():
+        for l in range(2):
+            start(w_copy(l, 2))
+        for g in range(3):
+            for half in range(2):
+                start(wx_copy(half, g))
+        for g in range(3):
+            for l in range(2):
+                arrived(w.at[l, stage_rows(g), stage_cols], s_recv.at[l, g])
+                start(forward_copy(l, g))
+        for g in range(3):
+            for l in range(2):
+                finish(w_copy(l, g))
+                finish(forward_copy(l, g))
+
     for k in range(1, CHUNKS):
         start(p_copy(k))
 
     @pl.when(hub)
     def _():
         first = layer == 0
+        for i in range(4):
+            arrived(h0.at[i], z_recv.at[i])
         for b in range(2):
-            hid[0, b] = h0[layer, :, b * HALF:(b + 1) * HALF].astype(BF16)
-        state[...] = h0[layer, :, pl.ds(pl.multiple_of(core * HALF, HALF), HALF)]
+            hid[0, b] = jnp.concatenate([h0[2 * b], h0[2 * b + 1]], axis=1).astype(BF16)
+        state[...] = jnp.concatenate([h0[2 * core], h0[2 * core + 1]], axis=1)
 
         @pl.when(jnp.logical_not(first))
         def _():
@@ -102,9 +205,22 @@
                 return carry
             lax.fori_loop(0, STEPS, clear, 0)
 
-        for s in range(2):
+        def weights_in(s, b, g, h, rows):
+            at = pl.ds(b * ROWS + h * (ROWS // 2), rows)
+            arrived(w.at[s, at, gate_cols(g)], w_recv.at[s, b, g, h])
+
+        for g in range(3):
             for b in range(2):
-                arrived(w.at[s, pl.ds(b * ROWS, ROWS)], w_recv.at[s, b])
+                weights_in(1, b, g, 0, ROWS)
+
+                @pl.when(core == chip)
+                def _():
+                    weights_in(0, b, g, 0, ROWS)
+
+                @pl.when(core != chip)
+                def _():
+                    for h in range(2):
+                        weights_in(0, b, g, h, ROWS // 2)
 
         def partner(t):
             return remote(hid.at[t, core], hid.at[t, core], n_send.at[t % RING], h_recv.at[t, core],
@@ -235,8 +351,9 @@
 
     @pl.when(jnp.logical_not(hub))
     def _():
-        for i in range(4):
-            arrived(w.at[i // 2, pl.ds((i % 2) * ROWS, ROWS), pl.ds(0, 3 * PART)], wx_recv.at[i])
+        for g in range(3):
+            for i in range(4):
+                arrived(w.at[i // 2, pl.ds((i % 2) * ROWS, ROWS), pl.ds(g * PART, PART)], wx_recv.at[i, g])
 
         def project(t):
             return remote(pbuf.at[0, core, t], pbuf.at[0, core, t], h_send.at[t % RING, 0, 0],
@@ -247,7 +364,8 @@
                 arrived(hid.at[t + 1, b], h_recv.at[t + 1, b])
             total = jnp.dot(hid[t + 1, 0], w[0, :, 0:3 * PART], preferred_element_type=F32)
             total = total + jnp.dot(hid[t + 1, 1], w[1, :, 0:3 * PART], preferred_element_type=F32)
-            pbuf[0, core, t] = total + bias[...]
+            shift = jnp.concatenate([bias_of(bias2, g) for g in range(3)], axis=1)
+            pbuf[0, core, t] = total + shift
 
             @pl.when(t >= RING)
             def _():
@@ -260,8 +378,24 @@
             project(t).wait_send()
 
     for l in range(2):
-        finish(w_copy(l))
-        finish(wx_copy(l))
+        @pl.when(hub & (chip == l))
+        def _():
+            for g in range(3):
+                finish(w_copy(l, g))
+                if l == 0:
+                    for half in range(2):
+                        finish(wx_copy(half, g))
+
+    @pl.when(jnp.logical_not(hub))
+    def _():
+        for g in range(3):
+            for half in range(2):
+                finish(wx_copy(half, g))
+    finish(x_copy(other))
+    for g in range(3):
+        finish(wx1_copy(other, g))
+    for to in range(2):
+        finish(h0_copy(to))
     for k in range(CHUNKS):
         finish(p_copy(k))
     for l in range(2):
@@ -282,18 +416,22 @@
     fin_out[...] = finbuf[...]
 
 
-def gru_call(w_in, wx_in, p_in, h0, bias):
+def gru_call(*operands):
     dma = pltpu.SemaphoreType.DMA
     any_spec = pl.BlockSpec(memory_space=pl.ANY)
     vmem_spec = pl.BlockSpec(memory_space=pltpu.VMEM)
     return pl.pallas_call(
         gru_kernel,
         out_shape=(jax.ShapeDtypeStruct((STEPS, BATCH, OWN), BF16), jax.ShapeDtypeStruct((2, BATCH, OWN), F32)),
-        in_specs=[any_spec, any_spec, any_spec, vmem_spec, vmem_spec],
+        in_specs=[any_spec] * 7 + [vmem_spec] * 3,
         out_specs=(vmem_spec, vmem_spec),
         scratch_shapes=[
             pltpu.VMEM((2, HALF, 3 * HALF), BF16),
             pltpu.VMEM((2, 2, STEPS, BATCH, 3 * PART), F32),
+            pltpu.VMEM((STEPS, BATCH, 3 * PART), F32),
+            pltpu.VMEM((STEPS * BATCH, 2 * ROWS), BF16),
+            pltpu.VMEM((2 * ROWS, 3 * PART), BF16),
+            pltpu.VMEM((4, BATCH, ROWS), F32),
             pltpu.VMEM((STEPS + 1, 2, BATCH, HALF), BF16),
             pltpu.VMEM((2, 2, BATCH, HALF), BF16),
             pltpu.VMEM((BATCH, HALF), F32),
@@ -301,8 +439,11 @@
             pltpu.VMEM((STEPS, BATCH, OWN), BF16),
             pltpu.VMEM((4, BATCH, OWN), F32),
             pltpu.VMEM((2, BATCH, OWN), F32),
-            dma((2,)), dma((2, 2)),
+            dma((1,)), dma((2,)), dma((3,)), dma((2, 3)),
             dma((2,)), dma((4,)),
+            dma((2, 3)), dma((2, 3)), dma((2, 3)),
+            dma((2, 3)), dma((2, 2, 3, 2)),
+            dma((2, 3)), dma((4, 3)),
             dma((CHUNKS,)), dma((STEPS, 2, 2)),
             dma((RING, 2, 2)), dma((STEPS + 1, 2)),
             dma((RING,)), dma((2,)), dma((2,)),
@@ -311,7 +452,7 @@
         ],
         compiler_params=pltpu.CompilerParams(has_side_effects=True, vmem_limit_bytes=62 * 2**20),
         name="gru",
-    )(w_in, wx_in, p_in, h0, bias)
+    )(*operands)
 
 
 def solution(mesh):
@@ -320,33 +461,14 @@
     wide_spec = P("row", None, "col")
     square_spec = P("row", "col")
     bias_spec = P(None, "col")
-    swap = [(0, 1), (1, 0), (2, 3), (3, 2)]
-
-    def halves(w):
-        return w.reshape(ROWS, 3, 2, PART).transpose(2, 0, 1, 3).reshape(2, ROWS, 3 * PART)
 
     def device_body(x_rows, h_rows, wx_l1, whru_l1, whn_l1, bias_l1, wx_l2, whru_l2, whn_l2, bias_l2):
-        row = lax.axis_index("row")
-        core = row % 2
-        chip = row // 2
-
-        def bias_half(b):
-            return lax.dynamic_index_in_dim(b.reshape(3, 2, PART), core, 1, keepdims=False).reshape(1, 3 * PART)
-
-        wx1 = halves(wx_l1)
-        own = lax.dynamic_index_in_dim(wx1, core, 0, keepdims=False)
-        theirs = lax.ppermute(lax.dynamic_index_in_dim(wx1, 1 - core, 0, keepdims=False), "row", swap)
-        x_own = x_rows.reshape(STEPS * BATCH, ROWS)
-        x_theirs = lax.ppermute(x_own, "row", swap)
-        p1 = jnp.dot(x_own, own, preferred_element_type=F32) + jnp.dot(x_theirs, theirs, preferred_element_type=F32)
-        p1 = p1 + jnp.where(chip == 0, bias_half(bias_l1), 0.0)
-        p1 = p1.reshape(STEPS, BATCH, 3 * PART)
-
-        h0 = lax.all_gather(h_rows, "row", axis=2, tiled=True)
-        w_rec = jnp.stack([
-            jnp.concatenate([whru_l1.reshape(ROWS, 2 * HALF), whn_l1], axis=1),
-            jnp.concatenate([whru_l2.reshape(ROWS, 2 * HALF), whn_l2], axis=1)])
-        return gru_call(w_rec, halves(wx_l2), p1, h0, bias_half(bias_l2))
+        def by_gate(weights):
+            return weights.transpose(1, 0, 2)
+
+        return gru_call(
+            x_rows.reshape(STEPS * BATCH, ROWS), by_gate(wx_l1), by_gate(wx_l2), by_gate(whru_l1), by_gate(whru_l2),
+            whn_l1, whn_l2, h_rows, bias_l1, bias_l2)
 
     return jax.shard_map(
         device_body,

time: 632 us -> 507 us (0.80)
  Pallas kernels: 547 us -> 497 us
  local copies, waits for them, and re-layouts: 48.1 us -> 9.63 us
  matrix products: 12.5 us -> 0 us
  other arithmetic: 12.5 us -> 0 us
  blocking collectives: 10 us -> 0 us
    pallas_call x1, Pallas kernels: 547 us -> 497 us  [gru_call(): pl.pallas_call(gru_kernel, out_shape=(jax.ShapeDtypeStruct((STEPS, BATCH,...]
    unnamed x22 -> x2, local copies, waits for them, and re-layouts: 26.8 us -> 3.13 us
    dot_general x2 -> x0, matrix products: 12.5 us -> none  [the longest x1 6.74 us: device_body(): jnp.dot(x_theirs, theirs, preferred_element_type=F32)]
    another operation x2 -> x0, other arithmetic: 12.5 us -> none  [device_body(): jnp.stack([jnp.concatenate([whru_l1.reshape(ROWS, 2 * HALF), whn_l1], axi...]
    all_gather x1 -> x0, blocking collectives: 10 us -> none  [device_body(): h0 = lax.all_gather(h_rows, 'row', axis=2, tiled=True)]
    reshape x2 -> x0, local copies, waits for them, and re-layouts: 7.95 us -> none  [the longest x1 7.93 us: halves(): w.reshape(ROWS, 3, 2, PART).transpose(2, 0, 1, 3).reshape(2, ROWS, 3 * PART)]
  transfers between devices with their start and end apart: 2 -> 0, of which waited for: 0 -> 0; matrix products, arithmetic and copies ran while one was open for 7% -> 0% of each run, Pallas kernels for 0% -> 0%
where the time goes in v2:
time: 507 us
  Pallas kernels  497 us (98%)
  local copies, waits for them, and re-layouts  9.63 us (2%)
    pallas_call x1, Pallas kernels, gru_call(): pl.pallas_call(gru_kernel, out_shape=(jax.ShapeDtypeStruct((STEPS, BATCH,...  497 us

profile of v2, /device:TPU:0, one launch (start us, length us, event | category | flops | bytes accessed | tf_op | source)
XLA Modules:
  0.0 507.2 jit_solution(10304554307373662839)
XLA Ops:
  0.6 6.5 %copy_bitcast_fusion = (bf16[2,640,1280]{2,1,0:T(8,128)(2,1)}, bf16[2,640,1280]{2,1,0:T(8,128)(2,1)}) fusion(bf16[640,2,1280]{2,1,0:T(2,128)(2,1)} %param.17, bf16[640,2,1280]{2,1,0:T(2,128)(2,1)} %param.13), kind=kLoop, calls=%fused_computation | loop fusion | bytes 13107200 | tf_op jit(solution)/shard_map/transpose | solution.py:467
  7.1 496.9 %gru.1 = (bf16[64,8,320]{2,1,0:T(8,128)(2,1)}, f32[2,8,320]{2,1,0:T(8,128)}) custom-call(bf16[512,640]{1,0:T(8,128)(2,1)} %bitcast.9, bf16[3,640,1280]{2,1,0:T(8,128)(2,1)} %bitcast.7, bf16[3,640,1280]{2,1,0:T(8,128)(2,1)} %bitcast.8, bf16[2,640,1280]{2,1,0:T(8,128)(2,1)} %get-tuple-element.3.ru1_in, bf16[2,640,1280]{2,1,0:T(8,128)(2,1)} %get-tuple-element.2.ru2_in, ...), custom_call_target="tpu_custom_call" | custom-call | tf_op jit(solution)/shard_map/gru/pallas_call | solution.py:423
  504.1 1.8 copy.18
  505.9 1.3 copy.19

commit v3 on v2

--- a/solution.py
+++ b/solution.py
@@ -19,13 +19,15 @@
 OWN = 320
 CHUNK = 8
 CHUNKS = STEPS // CHUNK
+LEAD = 4
+AHEAD = 12
 RING = 4
 
 
 def gru_kernel(x_in, wx1_in, wx2_in, ru1_in, ru2_in, n1_in, n2_in, h_in, bias1, bias2, seq_out, fin_out,
                w, pbuf, psrc, xs, wx1, h0, hid, rhb, state, outbuf, oscr, finsrc, finbuf,
                x_send, x_recv, v_send, v_recv, z_send, z_recv, s_send, s_recv, t_send,
-               w_send, w_recv, wx_send, wx_recv, p_send, p_recv, h_send, h_recv,
+               w_send, w_recv, wx_send, wx_recv, q_send, q_recv, b_send, b_recv, p_send, p_recv, h_send, h_recv,
                n_send, r_send, r_recv, o_send, o_recv, f_send, f_recv):
     row = lax.axis_index("row")
     col = lax.axis_index("col")
@@ -111,9 +113,32 @@
         return (wx2_in.at[g, :, pl.ds(half * PART, PART)], w.at[chip, my_rows, pl.ds(g * PART, PART)],
                 wx_send.at[half, g], wx_recv.at[row, g], 2 * (1 - col) + half, col)
 
-    def p_copy(k):
-        at = pl.ds(k * CHUNK, CHUNK)
-        return psrc.at[at], pbuf.at[chip, core, at], p_send.at[k], p_recv.at[k, chip, core], col, 0
+    def q_copy():
+        return psrc, pbuf.at[0, core], q_send.at[0], q_recv.at[core], 0, 0
+
+    def b_copy(t, steps):
+        at = pl.ds(t, steps)
+        return psrc.at[at], pbuf.at[1, core, at], b_send.at[t % AHEAD], b_recv.at[t], core, 1
+
+    def p_copy(t):
+        return psrc.at[t], pbuf.at[chip, core, t], p_send.at[t % RING], p_recv.at[t, core], col, 0
+
+    def send_p(t):
+        @pl.when(chip == 0)
+        def _():
+            @pl.when(t == 0)
+            def _():
+                arrived(pbuf.at[1, core, pl.ds(0, LEAD)], b_recv.at[0])
+
+            @pl.when(t == LEAD)
+            def _():
+                arrived(pbuf.at[1, core, pl.ds(LEAD, AHEAD - LEAD)], b_recv.at[LEAD])
+
+            @pl.when(t >= AHEAD)
+            def _():
+                arrived(pbuf.at[1, core, t], b_recv.at[t])
+            psrc[t] = psrc[t] + pbuf[1, core, t]
+        start(p_copy(t))
 
     for to in (core, other):
         start(x_copy(to))
@@ -153,14 +178,18 @@
         return carry
 
     lax.fori_loop(0, CHUNKS, project_x, 0)
-    start(p_copy(0))
 
     for l in range(2):
         @pl.when(hub & (chip == l))
         def _():
+            if l == 0:
+                start(q_copy())
             for g in range(3):
                 for h in range(2):
                     finish(stage_copy(l, h, g))
+            if l == 1:
+                start(b_copy(0, LEAD))
+                finish(b_copy(0, LEAD))
             for g in range(3):
                 for half in range(2):
                     start(wx_copy(half, g))
@@ -168,6 +197,7 @@
                 for g in range(3):
                     for half in range(2):
                         finish(wx_copy(half, g))
+                start(b_copy(LEAD, AHEAD - LEAD))
 
     @pl.when(jnp.logical_not(hub))
     def _():
@@ -180,13 +210,15 @@
             for l in range(2):
                 arrived(w.at[l, stage_rows(g), stage_cols], s_recv.at[l, g])
                 start(forward_copy(l, g))
+
+        def lead(t, carry):
+            send_p(t)
+            return carry
+        lax.fori_loop(0, LEAD, lead, 0)
         for g in range(3):
             for l in range(2):
                 finish(w_copy(l, g))
                 finish(forward_copy(l, g))
-
-    for k in range(1, CHUNKS):
-        start(p_copy(k))
 
     @pl.when(hub)
     def _():
@@ -197,7 +229,14 @@
             hid[0, b] = jnp.concatenate([h0[2 * b], h0[2 * b + 1]], axis=1).astype(BF16)
         state[...] = jnp.concatenate([h0[2 * core], h0[2 * core + 1]], axis=1)
 
-        @pl.when(jnp.logical_not(first))
+        joined = first & (core == 0)
+
+        @pl.when(joined)
+        def _():
+            for b in range(2):
+                arrived(pbuf.at[0, b], q_recv.at[b])
+
+        @pl.when(jnp.logical_not(joined))
         def _():
             def clear(t, carry):
                 for b in range(2):
@@ -243,18 +282,8 @@
                 [pbuf[0, b, t, :, cols] + pbuf[1, b, t, :, cols] for b in range(2)], axis=1)
 
         def tick(t, carry):
-            @pl.when(first & (t % CHUNK == 0))
-            def _():
-                k = t // CHUNK
-                at = pl.ds(k * CHUNK, CHUNK)
-                for a in range(2):
-                    for b in range(2):
-                        arrived(pbuf.at[a, b, at], p_recv.at[k, a, b])
-
-            @pl.when(jnp.logical_not(first))
-            def _():
-                for b in range(2):
-                    arrived(pbuf.at[0, b, t], p_recv.at[t, 0, b])
+            for b in range(2):
+                arrived(pbuf.at[jnp.where(joined, 1, 0), b, t], p_recv.at[t, b])
 
             ru_own = jnp.dot(hid[t, core], w[0, :, 0:2 * HALF], preferred_element_type=F32)
 
@@ -299,6 +328,17 @@
                 for i in range(4):
                     outbuf[i, t] = h_bf[:, i * OWN:(i + 1) * OWN]
 
+                @pl.when(t + AHEAD < STEPS)
+                def _():
+                    @pl.when(t == 1)
+                    def _():
+                        finish(b_copy(LEAD, AHEAD - LEAD))
+
+                    @pl.when(t > 0)
+                    def _():
+                        finish(b_copy(t - 1 + AHEAD, 1))
+                    start(b_copy(t + AHEAD, 1))
+
                 @pl.when(t % CHUNK == CHUNK - 1)
                 def _():
                     for i in range(4):
@@ -357,7 +397,7 @@
 
         def project(t):
             return remote(pbuf.at[0, core, t], pbuf.at[0, core, t], h_send.at[t % RING, 0, 0],
-                          p_recv.at[t, 0, core], 2 + col, 1)
+                          p_recv.at[t, core], 2 + col, 1)
 
         def tick(t, carry):
             for b in range(2):
@@ -371,11 +411,17 @@
             def _():
                 project(t - RING).wait_send()
             project(t).start()
+
+            @pl.when(t + LEAD < STEPS)
+            def _():
+                finish(p_copy(t))
+                send_p(t + LEAD)
             return carry
 
         lax.fori_loop(0, STEPS, tick, 0)
         for t in range(STEPS - RING, STEPS):
             project(t).wait_send()
+            finish(p_copy(t))
 
     for l in range(2):
         @pl.when(hub & (chip == l))
@@ -385,6 +431,10 @@
                 if l == 0:
                     for half in range(2):
                         finish(wx_copy(half, g))
+            if l == 0:
+                finish(q_copy())
+            else:
+                finish(b_copy(STEPS - 1, 1))
 
     @pl.when(jnp.logical_not(hub))
     def _():
@@ -396,8 +446,6 @@
         finish(wx1_copy(other, g))
     for to in range(2):
         finish(h0_copy(to))
-    for k in range(CHUNKS):
-        finish(p_copy(k))
     for l in range(2):
         @pl.when(jnp.logical_not((row == 2 * l + col) & (col == l)))
         def _():
@@ -444,7 +492,8 @@
             dma((2, 3)), dma((2, 3)), dma((2, 3)),
             dma((2, 3)), dma((2, 2, 3, 2)),
             dma((2, 3)), dma((4, 3)),
-            dma((CHUNKS,)), dma((STEPS, 2, 2)),
+            dma((1,)), dma((2,)), dma((AHEAD,)), dma((STEPS,)),
+            dma((RING,)), dma((STEPS, 2)),
             dma((RING, 2, 2)), dma((STEPS + 1, 2)),
             dma((RING,)), dma((2,)), dma((2,)),
             dma((4, CHUNKS)), dma((CHUNKS,)),

time: 507 us -> 419 us (0.83)
  Pallas kernels: 497 us -> 409 us
    pallas_call x1, Pallas kernels: 497 us -> 409 us  [gru_call(): pl.pallas_call(gru_kernel, out_shape=(jax.ShapeDtypeStruct((STEPS, BATCH,...]
where the time goes in v3:
time: 419 us
  Pallas kernels  409 us (98%)
  local copies, waits for them, and re-layouts  9.63 us (2%)
    pallas_call x1, Pallas kernels, gru_call(): pl.pallas_call(gru_kernel, out_shape=(jax.ShapeDtypeStruct((STEPS, BATCH,...  409 us

profile of v3, /device:TPU:0, one launch (start us, length us, event | category | flops | bytes accessed | tf_op | source)
XLA Modules:
  0.0 419.0 jit_solution(614405175194906717)
XLA Ops:
  0.6 6.5 %copy_bitcast_fusion = (bf16[2,640,1280]{2,1,0:T(8,128)(2,1)}, bf16[2,640,1280]{2,1,0:T(8,128)(2,1)}) fusion(bf16[640,2,1280]{2,1,0:T(2,128)(2,1)} %param.17, bf16[640,2,1280]{2,1,0:T(2,128)(2,1)} %param.13), kind=kLoop, calls=%fused_computation | loop fusion | bytes 13107200 | tf_op jit(solution)/shard_map/transpose | solution.py:516
  7.1 408.7 %gru.1 = (bf16[64,8,320]{2,1,0:T(8,128)(2,1)}, f32[2,8,320]{2,1,0:T(8,128)}) custom-call(bf16[512,640]{1,0:T(8,128)(2,1)} %bitcast.9, bf16[3,640,1280]{2,1,0:T(8,128)(2,1)} %bitcast.7, bf16[3,640,1280]{2,1,0:T(8,128)(2,1)} %bitcast.8, bf16[2,640,1280]{2,1,0:T(8,128)(2,1)} %get-tuple-element.3.ru1_in, bf16[2,640,1280]{2,1,0:T(8,128)(2,1)} %get-tuple-element.2.ru2_in, ...), custom_call_target="tpu_custom_call" | custom-call | tf_op jit(solution)/shard_map/gru/pallas_call | solution.py:471
  415.8 1.8 copy.18
  417.6 1.3 copy.19

commit v4 on v3

--- a/solution.py
+++ b/solution.py
@@ -22,6 +22,7 @@
 LEAD = 4
 AHEAD = 12
 RING = 4
+CUT = (0, 768, HALF)
 
 
 def gru_kernel(x_in, wx1_in, wx2_in, ru1_in, ru2_in, n1_in, n2_in, h_in, bias1, bias2, seq_out, fin_out,
@@ -261,12 +262,19 @@
                     for h in range(2):
                         weights_in(0, b, g, h, ROWS // 2)
 
-        def partner(t):
-            return remote(hid.at[t, core], hid.at[t, core], n_send.at[t % RING], h_recv.at[t, core],
-                          2 * chip + other, col)
+        def cut(i):
+            return pl.ds(CUT[i], CUT[i + 1] - CUT[i])
+
+        def partner(t, i):
+            piece = hid.at[t, core, :, cut(i)]
+            return remote(piece, piece, n_send.at[t % RING, i], h_recv.at[t, core, i], 2 * chip + other, col)
+
+        def swap(q, i):
+            piece = rhb.at[q, core, :, cut(i)]
+            return remote(piece, piece, r_send.at[q, i], r_recv.at[q, i], 2 * chip + other, col)
 
         def helper(t, y, b):
-            return remote(hid.at[t, core], hid.at[t, core], h_send.at[t % RING, y, b], h_recv.at[t, core],
+            return remote(hid.at[t, core], hid.at[t, core], h_send.at[t % RING, y, b], h_recv.at[t, core, 0],
                           2 * (1 - y) + b, y)
 
         def piece(i, k):
@@ -285,34 +293,56 @@
             for b in range(2):
                 arrived(pbuf.at[jnp.where(joined, 1, 0), b, t], p_recv.at[t, b])
 
-            ru_own = jnp.dot(hid[t, core], w[0, :, 0:2 * HALF], preferred_element_type=F32)
+            q = t % 2
+            lo = [slice(CUT[i], CUT[i + 1]) for i in range(2)]
+
+            def dot(vec, mat):
+                return jnp.dot(vec, mat, preferred_element_type=F32)
+
+            def columns(g, i):
+                return slice(g * HALF + CUT[i], g * HALF + CUT[i + 1])
+
+            def sigmoid(v):
+                return 0.5 * jnp.tanh(0.5 * v) + 0.5
+
+            p_n = gate(t, 2)
+            ru_own = dot(hid[t, core], w[0, :, 0:2 * HALF])
+            r_base = gate(t, 0) + ru_own[:, 0:HALF]
+            u_base = gate(t, 1) + ru_own[:, HALF:]
 
             @pl.when(t > 0)
             def _():
-                partner(t).wait_send()
-                arrived(hid.at[t, other], h_recv.at[t, other])
-
-            r_sum = ru_own[:, 0:HALF] + jnp.dot(hid[t, other], w[1, :, 0:HALF], preferred_element_type=F32)
-            reset = jax.nn.sigmoid(gate(t, 0) + r_sum)
-            q = t % 2
-            rhb[q, core] = (reset * state[...]).astype(BF16)
-            swap = remote(rhb.at[q, core], rhb.at[q, core], r_send.at[q], r_recv.at[q], 2 * chip + other, col)
-            swap.start()
-            u_sum = ru_own[:, HALF:] + jnp.dot(hid[t, other], w[1, :, HALF:2 * HALF], preferred_element_type=F32)
-            update = jax.nn.sigmoid(gate(t, 1) + u_sum)
-            n_sum = gate(t, 2) + jnp.dot(rhb[q, core], w[0, :, 2 * HALF:], preferred_element_type=F32)
-            swap.wait_send()
-            arrived(rhb.at[q, other], r_recv.at[q])
-            n_sum = n_sum + jnp.dot(rhb[q, other], w[1, :, 2 * HALF:], preferred_element_type=F32)
-            cand = jnp.tanh(n_sum)
-            h_next = (1.0 - update) * cand + update * state[...]
-            state[...] = h_next
-            h_bf = h_next.astype(BF16)
-            hid[t + 1, core] = h_bf
-
-            @pl.when(t < STEPS - 1)
-            def _():
-                partner(t + 1).start()
+                for i in range(2):
+                    partner(t, i).wait_send()
+                    arrived(hid.at[t, other, :, cut(i)], h_recv.at[t, other, i])
+
+            h_other = hid[t, other]
+            r_oth = [dot(h_other, w[1, :, columns(0, i)]) for i in range(2)]
+            u_oth = [None, None]
+            for i in range(2):
+                reset = sigmoid(r_base[:, lo[i]] + r_oth[i])
+                rhb[q, core, :, lo[i]] = (reset * state[:, lo[i]]).astype(BF16)
+                swap(q, i).start()
+                u_oth[1 - i] = dot(h_other, w[1, :, columns(1, 1 - i)])
+            update = [sigmoid(u_base[:, lo[i]] + u_oth[i]) for i in range(2)]
+            n_own = p_n + dot(rhb[q, core], w[0, :, 2 * HALF:])
+            swap(q, 0).wait_send()
+            arrived(rhb.at[q, other, :, cut(0)], r_recv.at[q, 0])
+            n_own = n_own + dot(rhb[q, other, :, lo[0]], w[1, lo[0], 2 * HALF:])
+            swap(q, 1).wait_send()
+            arrived(rhb.at[q, other, :, cut(1)], r_recv.at[q, 1])
+            n_oth = [dot(rhb[q, other, :, lo[1]], w[1, lo[1], columns(2, i)]) for i in range(2)]
+            h_parts = []
+            for i in range(2):
+                cand = jnp.tanh(n_own[:, lo[i]] + n_oth[i])
+                h_next = (1.0 - update[i]) * cand + update[i] * state[:, lo[i]]
+                state[:, lo[i]] = h_next
+                h_parts.append(h_next.astype(BF16))
+                hid[t + 1, core, :, lo[i]] = h_parts[i]
+
+                @pl.when(t < STEPS - 1)
+                def _():
+                    partner(t + 1, i).start()
 
             @pl.when(first)
             def _():
@@ -325,6 +355,7 @@
 
             @pl.when(jnp.logical_not(first))
             def _():
+                h_bf = jnp.concatenate(h_parts, axis=1)
                 for i in range(4):
                     outbuf[i, t] = h_bf[:, i * OWN:(i + 1) * OWN]
 
@@ -401,7 +432,7 @@
 
         def tick(t, carry):
             for b in range(2):
-                arrived(hid.at[t + 1, b], h_recv.at[t + 1, b])
+                arrived(hid.at[t + 1, b], h_recv.at[t + 1, b, 0])
             total = jnp.dot(hid[t + 1, 0], w[0, :, 0:3 * PART], preferred_element_type=F32)
             total = total + jnp.dot(hid[t + 1, 1], w[1, :, 0:3 * PART], preferred_element_type=F32)
             shift = jnp.concatenate([bias_of(bias2, g) for g in range(3)], axis=1)
@@ -494,8 +525,8 @@
             dma((2, 3)), dma((4, 3)),
             dma((1,)), dma((2,)), dma((AHEAD,)), dma((STEPS,)),
             dma((RING,)), dma((STEPS, 2)),
-            dma((RING, 2, 2)), dma((STEPS + 1, 2)),
-            dma((RING,)), dma((2,)), dma((2,)),
+            dma((RING, 2, 2)), dma((STEPS + 1, 2, 2)),
+            dma((RING, 2)), dma((2, 2)), dma((2, 2)),
             dma((4, CHUNKS)), dma((CHUNKS,)),
             dma((4,)), dma((2,)),
         ],

time: 419 us -> 407 us (0.971)
  Pallas kernels: 409 us -> 396 us
    pallas_call x1, Pallas kernels: 409 us -> 396 us  [gru_call(): pl.pallas_call(gru_kernel, out_shape=(jax.ShapeDtypeStruct((STEPS, BATCH,...]
where the time goes in v4:
time: 407 us; the launch traced here: 406 us
  Pallas kernels  396 us (97%)
  local copies, waits for them, and re-layouts  9.63 us (2%)
    pallas_call x1, Pallas kernels, gru_call(): pl.pallas_call(gru_kernel, out_shape=(jax.ShapeDtypeStruct((STEPS, BATCH,...  396 us

profile of v4, /device:TPU:0, one launch (start us, length us, event | category | flops | bytes accessed | tf_op | source)
XLA Modules:
  0.0 406.5 jit_solution(12550154970195009498)
XLA Ops:
  0.6 6.5 %copy_bitcast_fusion = (bf16[2,640,1280]{2,1,0:T(8,128)(2,1)}, bf16[2,640,1280]{2,1,0:T(8,128)(2,1)}) fusion(bf16[640,2,1280]{2,1,0:T(2,128)(2,1)} %param.17, bf16[640,2,1280]{2,1,0:T(2,128)(2,1)} %param.13), kind=kLoop, calls=%fused_computation | loop fusion | bytes 13107200 | tf_op jit(solution)/shard_map/transpose | solution.py:547
  7.1 396.2 %gru.1 = (bf16[64,8,320]{2,1,0:T(8,128)(2,1)}, f32[2,8,320]{2,1,0:T(8,128)}) custom-call(bf16[512,640]{1,0:T(8,128)(2,1)} %bitcast.9, bf16[3,640,1280]{2,1,0:T(8,128)(2,1)} %bitcast.7, bf16[3,640,1280]{2,1,0:T(8,128)(2,1)} %bitcast.8, bf16[2,640,1280]{2,1,0:T(8,128)(2,1)} %get-tuple-element.3.ru1_in, bf16[2,640,1280]{2,1,0:T(8,128)(2,1)} %get-tuple-element.2.ru2_in, ...), custom_call_target="tpu_custom_call" | custom-call | tf_op jit(solution)/shard_map/gru/pallas_call | solution.py:502
  403.4 1.8 copy.18
  405.1 1.3 copy.19

commit v5 on v4

--- a/solution.py
+++ b/solution.py
@@ -19,14 +19,14 @@
 OWN = 320
 CHUNK = 8
 CHUNKS = STEPS // CHUNK
-LEAD = 4
-AHEAD = 12
+LEAD = 5
+AHEAD = 9
 RING = 4
-CUT = (0, 768, HALF)
+CUT = (0, 512, HALF)
 
 
 def gru_kernel(x_in, wx1_in, wx2_in, ru1_in, ru2_in, n1_in, n2_in, h_in, bias1, bias2, seq_out, fin_out,
-               w, pbuf, psrc, xs, wx1, h0, hid, rhb, state, outbuf, oscr, finsrc, finbuf,
+               w, pbuf, psrc, xs, wx1, h0, hid, rhb, state, outbuf, finsrc,
                x_send, x_recv, v_send, v_recv, z_send, z_recv, s_send, s_recv, t_send,
                w_send, w_recv, wx_send, wx_recv, q_send, q_recv, b_send, b_recv, p_send, p_recv, h_send, h_recv,
                n_send, r_send, r_recv, o_send, o_recv, f_send, f_recv):
@@ -122,7 +122,7 @@
         return psrc.at[at], pbuf.at[1, core, at], b_send.at[t % AHEAD], b_recv.at[t], core, 1
 
     def p_copy(t):
-        return psrc.at[t], pbuf.at[chip, core, t], p_send.at[t % RING], p_recv.at[t, core], col, 0
+        return psrc.at[t], pbuf.at[chip, core, t], p_send.at[t % LEAD], p_recv.at[t, core], col, 0
 
     def send_p(t):
         @pl.when(chip == 0)
@@ -279,10 +279,7 @@
 
         def piece(i, k):
             at = pl.ds(k * CHUNK, CHUNK)
-            return remote(outbuf.at[i, at], oscr.at[at], o_send.at[i, k], o_recv.at[k], i, core)
-
-        def mine(i):
-            return (row == i) & (col == core)
+            return outbuf.at[i, at], seq_out.at[at], o_send.at[i, k], o_recv.at[k], i, core
 
         def gate(t, g):
             cols = pl.ds(g * PART, PART)
@@ -290,38 +287,41 @@
                 [pbuf[0, b, t, :, cols] + pbuf[1, b, t, :, cols] for b in range(2)], axis=1)
 
         def tick(t, carry):
+            q = t % 2
+            lo = [slice(CUT[i], CUT[i + 1]) for i in range(2)]
+
+            def dot(vec, mat):
+                return jnp.dot(vec, mat, preferred_element_type=F32)
+
+            def columns(g, i):
+                return slice(g * HALF + CUT[i], g * HALF + CUT[i + 1])
+
+            def sigmoid(v):
+                return 0.5 * jnp.tanh(0.5 * v) + 0.5
+
+            ru_own = dot(hid[t, core], w[0, :, 0:2 * HALF])
             for b in range(2):
                 arrived(pbuf.at[jnp.where(joined, 1, 0), b, t], p_recv.at[t, b])
 
-            q = t % 2
-            lo = [slice(CUT[i], CUT[i + 1]) for i in range(2)]
-
-            def dot(vec, mat):
-                return jnp.dot(vec, mat, preferred_element_type=F32)
-
-            def columns(g, i):
-                return slice(g * HALF + CUT[i], g * HALF + CUT[i + 1])
-
-            def sigmoid(v):
-                return 0.5 * jnp.tanh(0.5 * v) + 0.5
-
-            p_n = gate(t, 2)
-            ru_own = dot(hid[t, core], w[0, :, 0:2 * HALF])
-            r_base = gate(t, 0) + ru_own[:, 0:HALF]
-            u_base = gate(t, 1) + ru_own[:, HALF:]
-
-            @pl.when(t > 0)
-            def _():
-                for i in range(2):
+            def h_in_place(i):
+                @pl.when(t > 0)
+                def _():
                     partner(t, i).wait_send()
                     arrived(hid.at[t, other, :, cut(i)], h_recv.at[t, other, i])
 
+            h_in_place(0)
+            r_base = ru_own[:, 0:HALF] + dot(hid[t, other, :, lo[0]], w[1, lo[0], 0:HALF])
+            h_in_place(1)
+            r_base = gate(t, 0) + r_base
+            u_base = gate(t, 1) + ru_own[:, HALF:]
+            p_n = gate(t, 2)
             h_other = hid[t, other]
-            r_oth = [dot(h_other, w[1, :, columns(0, i)]) for i in range(2)]
+            r_oth = [dot(hid[t, other, :, lo[1]], w[1, lo[1], columns(0, i)]) for i in range(2)]
             u_oth = [None, None]
             for i in range(2):
-                reset = sigmoid(r_base[:, lo[i]] + r_oth[i])
-                rhb[q, core, :, lo[i]] = (reset * state[:, lo[i]]).astype(BF16)
+                h_half = 0.5 * state[:, lo[i]]
+                gated = h_half + h_half * jnp.tanh(0.5 * (r_base[:, lo[i]] + r_oth[i]))
+                rhb[q, core, :, lo[i]] = gated.astype(BF16)
                 swap(q, i).start()
                 u_oth[1 - i] = dot(h_other, w[1, :, columns(1, 1 - i)])
             update = [sigmoid(u_base[:, lo[i]] + u_oth[i]) for i in range(2)]
@@ -373,9 +373,7 @@
                 @pl.when(t % CHUNK == CHUNK - 1)
                 def _():
                     for i in range(4):
-                        @pl.when(jnp.logical_not(mine(i)))
-                        def _():
-                            piece(i, t // CHUNK).start()
+                        start(piece(i, t // CHUNK))
             return carry
 
         lax.fori_loop(0, STEPS, tick, 0)
@@ -385,33 +383,17 @@
             finsrc[i] = last[:, i * OWN:(i + 1) * OWN]
 
         def fin_copy(i):
-            return remote(finsrc.at[i], finbuf.at[layer], f_send.at[i], f_recv.at[layer], i, core)
+            return finsrc.at[i], fin_out.at[layer], f_send.at[i], f_recv.at[layer], i, core
 
         for i in range(4):
-            @pl.when(mine(i))
-            def _():
-                finbuf[layer] = finsrc[i]
-
-                @pl.when(jnp.logical_not(first))
-                def _():
-                    def take(t, carry):
-                        oscr[t] = outbuf[i, t]
-                        return carry
-                    lax.fori_loop(0, STEPS, take, 0)
-
-            @pl.when(jnp.logical_not(mine(i)))
-            def _():
-                fin_copy(i).start()
-
+            start(fin_copy(i))
         for i in range(4):
-            @pl.when(jnp.logical_not(mine(i)))
-            def _():
-                fin_copy(i).wait_send()
-
-                @pl.when(jnp.logical_not(first))
-                def _():
-                    for k in range(CHUNKS):
-                        piece(i, k).wait_send()
+            finish(fin_copy(i))
+
+            @pl.when(jnp.logical_not(first))
+            def _():
+                for k in range(CHUNKS):
+                    finish(piece(i, k))
 
         @pl.when(first)
         def _():
@@ -452,6 +434,7 @@
         lax.fori_loop(0, STEPS, tick, 0)
         for t in range(STEPS - RING, STEPS):
             project(t).wait_send()
+        for t in range(STEPS - LEAD, STEPS):
             finish(p_copy(t))
 
     for l in range(2):
@@ -478,21 +461,9 @@
     for to in range(2):
         finish(h0_copy(to))
     for l in range(2):
-        @pl.when(jnp.logical_not((row == 2 * l + col) & (col == l)))
-        def _():
-            arrived(finbuf.at[l], f_recv.at[l])
-
-    @pl.when(jnp.logical_not((row == 2 + col) & (col == 1)))
-    def _():
-        for k in range(CHUNKS):
-            at = pl.ds(k * CHUNK, CHUNK)
-            arrived(oscr.at[at], o_recv.at[k])
-
-    def emit(t, carry):
-        seq_out[t] = oscr[t]
-        return carry
-    lax.fori_loop(0, STEPS, emit, 0)
-    fin_out[...] = finbuf[...]
+        arrived(fin_out.at[l], f_recv.at[l])
+    for k in range(CHUNKS):
+        arrived(seq_out.at[pl.ds(k * CHUNK, CHUNK)], o_recv.at[k])
 
 
 def gru_call(*operands):
@@ -503,7 +474,7 @@
         gru_kernel,
         out_shape=(jax.ShapeDtypeStruct((STEPS, BATCH, OWN), BF16), jax.ShapeDtypeStruct((2, BATCH, OWN), F32)),
         in_specs=[any_spec] * 7 + [vmem_spec] * 3,
-        out_specs=(vmem_spec, vmem_spec),
+        out_specs=(any_spec, any_spec),
         scratch_shapes=[
             pltpu.VMEM((2, HALF, 3 * HALF), BF16),
             pltpu.VMEM((2, 2, STEPS, BATCH, 3 * PART), F32),
@@ -515,16 +486,14 @@
             pltpu.VMEM((2, 2, BATCH, HALF), BF16),
             pltpu.VMEM((BATCH, HALF), F32),
             pltpu.VMEM((4, STEPS, BATCH, OWN), BF16),
-            pltpu.VMEM((STEPS, BATCH, OWN), BF16),
             pltpu.VMEM((4, BATCH, OWN), F32),
-            pltpu.VMEM((2, BATCH, OWN), F32),
             dma((1,)), dma((2,)), dma((3,)), dma((2, 3)),
             dma((2,)), dma((4,)),
             dma((2, 3)), dma((2, 3)), dma((2, 3)),
             dma((2, 3)), dma((2, 2, 3, 2)),
             dma((2, 3)), dma((4, 3)),
             dma((1,)), dma((2,)), dma((AHEAD,)), dma((STEPS,)),
-            dma((RING,)), dma((STEPS, 2)),
+            dma((LEAD,)), dma((STEPS, 2)),
             dma((RING, 2, 2)), dma((STEPS + 1, 2, 2)),
             dma((RING, 2)), dma((2, 2)), dma((2, 2)),
             dma((4, CHUNKS)), dma((CHUNKS,)),

time: 407 us -> 399 us (0.980)
  Pallas kernels: 396 us -> 388 us
    pallas_call x1, Pallas kernels: 396 us -> 388 us  [gru_call(): pl.pallas_call(gru_kernel, out_shape=(jax.ShapeDtypeStruct((STEPS, BATCH,...]
where the time goes in v5:
time: 399 us; the launch traced here: 398 us
  Pallas kernels  388 us (97%)
  local copies, waits for them, and re-layouts  9.63 us (2%)
    pallas_call x1, Pallas kernels, gru_call(): pl.pallas_call(gru_kernel, out_shape=(jax.ShapeDtypeStruct((STEPS, BATCH,...  388 us

profile of v5, /device:TPU:0, one launch (start us, length us, event | category | flops | bytes accessed | tf_op | source)
XLA Modules:
  0.0 398.3 jit_solution(17078256703274174868)
XLA Ops:
  0.6 6.5 %copy_bitcast_fusion = (bf16[2,640,1280]{2,1,0:T(8,128)(2,1)}, bf16[2,640,1280]{2,1,0:T(8,128)(2,1)}) fusion(bf16[640,2,1280]{2,1,0:T(2,128)(2,1)} %param.17, bf16[640,2,1280]{2,1,0:T(2,128)(2,1)} %param.13), kind=kLoop, calls=%fused_computation | loop fusion | bytes 13107200 | tf_op jit(solution)/shard_map/transpose | solution.py:516
  7.1 388.0 %gru.1 = (bf16[64,8,320]{2,1,0:T(8,128)(2,1)}, f32[2,8,320]{2,1,0:T(8,128)}) custom-call(bf16[512,640]{1,0:T(8,128)(2,1)} %bitcast.9, bf16[3,640,1280]{2,1,0:T(8,128)(2,1)} %bitcast.7, bf16[3,640,1280]{2,1,0:T(8,128)(2,1)} %bitcast.8, bf16[2,640,1280]{2,1,0:T(8,128)(2,1)} %get-tuple-element.3.ru1_in, bf16[2,640,1280]{2,1,0:T(8,128)(2,1)} %get-tuple-element.2.ru2_in, ...), custom_call_target="tpu_custom_call" | custom-call | tf_op jit(solution)/shard_map/gru/pallas_call | solution.py:473
  395.1 1.8 copy.18
  396.9 1.3 copy.19

commit v6 on v5

--- a/solution.py
+++ b/solution.py
@@ -20,13 +20,14 @@
 CHUNK = 8
 CHUNKS = STEPS // CHUNK
 LEAD = 5
-AHEAD = 9
+AHEAD = 8
 RING = 4
+EARLY = 256
 CUT = (0, 512, HALF)
 
 
 def gru_kernel(x_in, wx1_in, wx2_in, ru1_in, ru2_in, n1_in, n2_in, h_in, bias1, bias2, seq_out, fin_out,
-               w, pbuf, psrc, xs, wx1, h0, hid, rhb, state, outbuf, finsrc,
+               w, pbuf, psrc, xs, wx1, h0, hid, rhb, state, early, outbuf, finsrc,
                x_send, x_recv, v_send, v_recv, z_send, z_recv, s_send, s_recv, t_send,
                w_send, w_recv, wx_send, wx_recv, q_send, q_recv, b_send, b_recv, p_send, p_recv, h_send, h_recv,
                n_send, r_send, r_recv, o_send, o_recv, f_send, f_recv):
@@ -286,6 +287,11 @@
             return jnp.concatenate(
                 [pbuf[0, b, t, :, cols] + pbuf[1, b, t, :, cols] for b in range(2)], axis=1)
 
+        def early_dot(t):
+            return jnp.dot(hid[t, core, :, 0:EARLY], w[0, 0:EARLY, 0:2 * HALF], preferred_element_type=F32)
+
+        early[...] = early_dot(0)
+
         def tick(t, carry):
             q = t % 2
             lo = [slice(CUT[i], CUT[i + 1]) for i in range(2)]
@@ -299,9 +305,18 @@
             def sigmoid(v):
                 return 0.5 * jnp.tanh(0.5 * v) + 0.5
 
-            ru_own = dot(hid[t, core], w[0, :, 0:2 * HALF])
+            ru_own = early[...] + dot(hid[t, core, :, EARLY:], w[0, EARLY:, 0:2 * HALF])
             for b in range(2):
                 arrived(pbuf.at[jnp.where(joined, 1, 0), b, t], p_recv.at[t, b])
+
+            @pl.when(first & (t > 0))
+            def _():
+                for y in range(2):
+                    for b in range(2):
+                        @pl.when(t > RING)
+                        def _():
+                            helper(t - RING, y, b).wait_send()
+                        helper(t, y, b).start()
 
             def h_in_place(i):
                 @pl.when(t > 0)
@@ -344,14 +359,8 @@
                 def _():
                     partner(t + 1, i).start()
 
-            @pl.when(first)
-            def _():
-                for y in range(2):
-                    for b in range(2):
-                        @pl.when(t >= RING)
-                        def _():
-                            helper(t + 1 - RING, y, b).wait_send()
-                        helper(t + 1, y, b).start()
+                if i == 0:
+                    early[...] = early_dot(t + 1)
 
             @pl.when(jnp.logical_not(first))
             def _():
@@ -397,6 +406,10 @@
 
         @pl.when(first)
         def _():
+            for y in range(2):
+                for b in range(2):
+                    helper(STEPS - RING, y, b).wait_send()
+                    helper(STEPS, y, b).start()
             for t in range(STEPS + 1 - RING, STEPS + 1):
                 for y in range(2):
                     for b in range(2):
@@ -485,6 +498,7 @@
             pltpu.VMEM((STEPS + 1, 2, BATCH, HALF), BF16),
             pltpu.VMEM((2, 2, BATCH, HALF), BF16),
             pltpu.VMEM((BATCH, HALF), F32),
+            pltpu.VMEM((BATCH, 2 * HALF), F32),
             pltpu.VMEM((4, STEPS, BATCH, OWN), BF16),
             pltpu.VMEM((4, BATCH, OWN), F32),
             dma((1,)), dma((2,)), dma((3,)), dma((2, 3)),

time: 399 us -> 392 us (0.982)
  Pallas kernels: 388 us -> 382 us
    pallas_call x1, Pallas kernels: 388 us -> 382 us  [gru_call(): pl.pallas_call(gru_kernel, out_shape=(jax.ShapeDtypeStruct((STEPS, BATCH,...]
where the time goes in v6:
time: 392 us
  Pallas kernels  382 us (97%)
  local copies, waits for them, and re-layouts  9.63 us (2%)
    pallas_call x1, Pallas kernels, gru_call(): pl.pallas_call(gru_kernel, out_shape=(jax.ShapeDtypeStruct((STEPS, BATCH,...  382 us

profile of v6, /device:TPU:0, one launch (start us, length us, event | category | flops | bytes accessed | tf_op | source)
XLA Modules:
  0.0 392.0 jit_solution(1301559722941219824)
XLA Ops:
  0.6 6.5 %copy_bitcast_fusion = (bf16[2,640,1280]{2,1,0:T(8,128)(2,1)}, bf16[2,640,1280]{2,1,0:T(8,128)(2,1)}) fusion(bf16[640,2,1280]{2,1,0:T(2,128)(2,1)} %param.17, bf16[640,2,1280]{2,1,0:T(2,128)(2,1)} %param.13), kind=kLoop, calls=%fused_computation | loop fusion | bytes 13107200 | tf_op jit(solution)/shard_map/transpose | solution.py:530
  7.1 381.8 %gru.1 = (bf16[64,8,320]{2,1,0:T(8,128)(2,1)}, f32[2,8,320]{2,1,0:T(8,128)}) custom-call(bf16[512,640]{1,0:T(8,128)(2,1)} %bitcast.9, bf16[3,640,1280]{2,1,0:T(8,128)(2,1)} %bitcast.7, bf16[3,640,1280]{2,1,0:T(8,128)(2,1)} %bitcast.8, bf16[2,640,1280]{2,1,0:T(8,128)(2,1)} %get-tuple-element.3.ru1_in, bf16[2,640,1280]{2,1,0:T(8,128)(2,1)} %get-tuple-element.2.ru2_in, ...), custom_call_target="tpu_custom_call" | custom-call | tf_op jit(solution)/shard_map/gru/pallas_call | solution.py:486
  388.9 1.8 copy.18
  390.7 1.3 copy.19

commit v7 on v6

--- a/solution.py
+++ b/solution.py
@@ -212,11 +212,13 @@
             for l in range(2):
                 arrived(w.at[l, stage_rows(g), stage_cols], s_recv.at[l, g])
                 start(forward_copy(l, g))
+            if g == 1:
+                send_p(jnp.int32(0))
 
         def lead(t, carry):
             send_p(t)
             return carry
-        lax.fori_loop(0, LEAD, lead, 0)
+        lax.fori_loop(1, LEAD, lead, 0)
         for g in range(3):
             for l in range(2):
                 finish(w_copy(l, g))
@@ -250,7 +252,7 @@
             at = pl.ds(b * ROWS + h * (ROWS // 2), rows)
             arrived(w.at[s, at, gate_cols(g)], w_recv.at[s, b, g, h])
 
-        for g in range(3):
+        def gate_in(g):
             for b in range(2):
                 weights_in(1, b, g, 0, ROWS)
 
@@ -263,6 +265,9 @@
                     for h in range(2):
                         weights_in(0, b, g, h, ROWS // 2)
 
+        gate_in(0)
+        gate_in(1)
+
         def cut(i):
             return pl.ds(CUT[i], CUT[i + 1] - CUT[i])
 
@@ -292,7 +297,7 @@
 
         early[...] = early_dot(0)
 
-        def tick(t, carry):
+        def tick(t, head):
             q = t % 2
             lo = [slice(CUT[i], CUT[i + 1]) for i in range(2)]
 
@@ -309,8 +314,9 @@
             for b in range(2):
                 arrived(pbuf.at[jnp.where(joined, 1, 0), b, t], p_recv.at[t, b])
 
-            @pl.when(first & (t > 0))
-            def _():
+            if not head:
+              @pl.when(first)
+              def _():
                 for y in range(2):
                     for b in range(2):
                         @pl.when(t > RING)
@@ -319,8 +325,7 @@
                         helper(t, y, b).start()
 
             def h_in_place(i):
-                @pl.when(t > 0)
-                def _():
+                if not head:
                     partner(t, i).wait_send()
                     arrived(hid.at[t, other, :, cut(i)], h_recv.at[t, other, i])
 
@@ -340,6 +345,8 @@
                 swap(q, i).start()
                 u_oth[1 - i] = dot(h_other, w[1, :, columns(1, 1 - i)])
             update = [sigmoid(u_base[:, lo[i]] + u_oth[i]) for i in range(2)]
+            if head:
+                gate_in(2)
             n_own = p_n + dot(rhb[q, core], w[0, :, 2 * HALF:])
             swap(q, 0).wait_send()
             arrived(rhb.at[q, other, :, cut(0)], r_recv.at[q, 0])
@@ -383,9 +390,13 @@
                 def _():
                     for i in range(4):
                         start(piece(i, t // CHUNK))
+
+        def later(t, carry):
+            tick(t, False)
             return carry
 
-        lax.fori_loop(0, STEPS, tick, 0)
+        tick(jnp.int32(0), True)
+        lax.fori_loop(1, STEPS, later, 0)
 
         last = state[...]
         for i in range(4):

time: 392 us -> 391 us (level)
  no operation moved by 1% of the time
where the time goes in v7:
time: 391 us
  Pallas kernels  381 us (97%)
  local copies, waits for them, and re-layouts  9.63 us (2%)
    pallas_call x1, Pallas kernels, gru_call(): pl.pallas_call(gru_kernel, out_shape=(jax.ShapeDtypeStruct((STEPS, BATCH,...  381 us

profile of v7, /device:TPU:0, one launch (start us, length us, event | category | flops | bytes accessed | tf_op | source)
XLA Modules:
  0.0 391.0 jit_solution(2520387352705860928)
XLA Ops:
  0.6 6.5 %copy_bitcast_fusion = (bf16[2,640,1280]{2,1,0:T(8,128)(2,1)}, bf16[2,640,1280]{2,1,0:T(8,128)(2,1)}) fusion(bf16[640,2,1280]{2,1,0:T(2,128)(2,1)} %param.17, bf16[640,2,1280]{2,1,0:T(2,128)(2,1)} %param.13), kind=kLoop, calls=%fused_computation | loop fusion | bytes 13107200 | tf_op jit(solution)/shard_map/transpose | solution.py:541
  7.1 380.8 %gru.1 = (bf16[64,8,320]{2,1,0:T(8,128)(2,1)}, f32[2,8,320]{2,1,0:T(8,128)}) custom-call(bf16[512,640]{1,0:T(8,128)(2,1)} %bitcast.9, bf16[3,640,1280]{2,1,0:T(8,128)(2,1)} %bitcast.7, bf16[3,640,1280]{2,1,0:T(8,128)(2,1)} %bitcast.8, bf16[2,640,1280]{2,1,0:T(8,128)(2,1)} %get-tuple-element.3.ru1_in, bf16[2,640,1280]{2,1,0:T(8,128)(2,1)} %get-tuple-element.2.ru2_in, ...), custom_call_target="tpu_custom_call" | custom-call | tf_op jit(solution)/shard_map/gru/pallas_call | solution.py:497
  387.9 1.8 copy.18
  389.7 1.3 copy.19
